TPU v7x, 256 devices: a whole 4x4x8 slice. The times are simulated.
256 devices in a mesh: dp: 64 (over z, y, core), mp: 4 (over x).
Axes of the slice: x: 4, y: 4, z: 8, core: 2. Of those that a mesh axis runs over, the one named last changes fastest.
Arguments:
- tokens: bfloat16 [393216, 512], P('dp'), may hold values from -6 to 6
- w_uvqk: bfloat16 [512, 2048], P(None, 'mp')
- w_out: bfloat16 [512, 512], replicated, may hold values from -0.25 to 0.25
- hist_len: int32 [64, 24], P('dp'), may hold values from 64 to 256, as said below
- owner: int32 [64, 24], P('dp'), may hold values from 0 to 63, as said below
- recv_offset: int32 [64, 24], P('dp'), may hold values from 0 to 47, as said below
- block_start: int32 [64, 24], P('dp'), may hold values from 0 to 47, as said below
Outputs:
- packed_out: bfloat16 [393216, 512], P('dp', 'mp')
- user_state: bfloat16 [1536, 512], P('dp', 'mp')
Inputs may be any that keep to these rules, and one draw needn't show every extreme that they name: User (d, u) has ceil(hist_len / 128) blocks, at most 2. owner[d, u] = (p(d) + r(u mod 64)) mod 64 for two permutations p, r of the indices of dp drawn from the seed: every owner receives exactly 24 users, and one device sends at most 1 users to one owner. On some owner every received user has 2 blocks. `recv_offset`: the users of one owner occupy disjoint runs of its 48 blocks, in the order of u; on some owner they fill all 48 blocks. `block_start`: the users of one device occupy disjoint runs of its 48 blocks, in the order of u.
All inputs are finite; a program needn't handle non-finite values.
Results may differ from a plain program's by a relative error of at most 0.0059.
Values may be sent and summed in bfloat16 or wider, within the bound.
No kernel may reach another device: no remote copies, remote signals or barrier semaphores. Data moves between devices by JAX's collectives and lax.ppermute only.
A program may use at most 128 MiB of HBM per device.

v0:
```python
import jax
import jax.numpy as jnp
from jax import lax
from jax.experimental import pallas as pl
from jax.experimental.pallas import tpu as pltpu
from jax.sharding import PartitionSpec as P

D = 512
HEADS = 4
HEAD = D // HEADS
BLOCK = 128
MAXB = 2
BLK_DEV = 48
USERS = 24
N_DP = 64
N_MP = 4
WIN = MAXB * BLOCK
MINE = USERS // N_MP
RAW = 2
DONE = MINE - RAW
TILE = 8
GROUPS = WIN // TILE
HALVES = N_DP // GROUPS
GROUP = 2
OWN_GROUP = 2
CHUNKS = 4
RAW_MSG = N_MP + 1
ROUND = DONE // HALVES
MSG = (ROUND + 1) * N_MP
EPS = 1e-05
BF16 = jnp.bfloat16
F32 = jnp.float32


def silu_of_twice(h):
    return h + h * jnp.tanh(h)


def project(half_parts, w_parts):
    acc = jnp.dot(half_parts[0], w_parts[0], preferred_element_type=F32)
    for n, w in zip(half_parts[1:], w_parts[1:]):
        acc = acc + jnp.dot(n, w, preferred_element_type=F32)
    proj = silu_of_twice(acc).astype(BF16)
    return [proj[:, j * HEAD : (j + 1) * HEAD] for j in range(4)]


def attend(q, k, v):
    row = lax.broadcasted_iota(jnp.int32, (BLOCK, BLOCK), 0)
    col = lax.broadcasted_iota(jnp.int32, (BLOCK, BLOCK), 1)
    causal = col <= row
    scale = 0.5 * HEAD ** (-0.5)
    contract_last = (((1,), (1,)), ((), ()))
    s0 = lax.dot_general(q[:BLOCK], k[:BLOCK], contract_last, preferred_element_type=F32)
    s1 = lax.dot_general(q[BLOCK:], k, contract_last, preferred_element_type=F32)
    a0 = jnp.where(causal, silu_of_twice(s0 * scale), 0.0).astype(BF16)
    b = silu_of_twice(s1 * scale)
    a1 = jnp.concatenate(
        [b[:, :BLOCK].astype(BF16), jnp.where(causal, b[:, BLOCK:], 0.0).astype(BF16)], axis=1
    )
    return jnp.concatenate(
        [
            jnp.dot(a0, v[:BLOCK], preferred_element_type=F32),
            jnp.dot(a1, v, preferred_element_type=F32),
        ],
        axis=0,
    )


def norm_stats(total, squares, unit=1.0):
    mean = total * (1.0 / D)
    var = squares * (1.0 / D) - mean * mean
    return mean, lax.rsqrt(var * (unit * unit) + EPS) * unit


def token_copies(tokens_ref, block, x_ref, row, sem):
    second = jnp.minimum(block + 1, BLK_DEV - 1)
    return [
        pltpu.make_async_copy(
            tokens_ref.at[pl.ds(b * BLOCK, BLOCK)],
            x_ref.at[pl.ds(row + j * BLOCK, BLOCK)],
            sem.at[j],
        )
        for j, b in enumerate((block, second))
    ]


def norm_half(x):
    mean, inv = norm_stats(
        jnp.sum(x, axis=1, keepdims=True), jnp.sum(x * x, axis=1, keepdims=True)
    )
    return ((x - mean) * (inv * 0.5)).astype(BF16)


def own_head_kernel(
    start_ref, part_ref, tokens_ref, w_ref, half_ref, att_ref, gate_ref,
    x_s, half_s, att_s, gate_s, w_s, sem_in, sem_w, sem_out,
):
    load_w = pltpu.make_async_copy(w_ref, w_s, sem_w)

    def loads(i):
        block = start_ref[0, part_ref[0] * MINE + RAW + i]
        return token_copies(tokens_ref, block, x_s, i * WIN, sem_in.at[i])

    def sends(step):
        rows = pl.ds(step * OWN_GROUP * WIN, OWN_GROUP * WIN)
        pairs = ((half_s, half_ref), (att_s, att_ref), (gate_s, gate_ref))
        return [
            pltpu.make_async_copy(a.at[rows], b.at[rows], sem_out.at[step, j])
            for j, (a, b) in enumerate(pairs)
        ]

    for i in range(DONE):
        for copy in loads(i):
            copy.start()
        if i == OWN_GROUP - 1:
            load_w.start()

    def group(step, carry):
        for j in range(OWN_GROUP):
            for copy in loads(step * OWN_GROUP + j):
                copy.wait()
        rows = pl.ds(pl.multiple_of(step * OWN_GROUP * WIN, WIN), OWN_GROUP * WIN)
        half = norm_half(x_s[rows, :].astype(F32))
        half_s[rows, :] = half

        @pl.when(step == 0)
        def _():
            load_w.wait()

        u, v, q, k = project([half], [w_s[...]])
        gate_s[rows, :] = u
        att_s[rows, :] = attend_users(OWN_GROUP, q, k, v)
        for copy in sends(step):
            copy.start()
        return carry

    lax.fori_loop(0, DONE // OWN_GROUP, group, 0)
    for step in range(DONE // OWN_GROUP):
        for copy in sends(step):
            copy.wait()


def in_vmem():
    return pl.BlockSpec(memory_space=pltpu.VMEM)


def in_hbm():
    return pl.BlockSpec(memory_space=pltpu.HBM)


def keep(array):
    return pltpu.with_memory_space_constraint(array, pltpu.VMEM)


def own_head(tokens, starts, part, w_own):
    kept = [((DONE * WIN, D), BF16), ((DONE * WIN, HEAD), F32), ((DONE * WIN, HEAD), BF16)]
    return pl.pallas_call(
        own_head_kernel,
        grid_spec=pltpu.PrefetchScalarGridSpec(
            num_scalar_prefetch=2,
            grid=(1,),
            in_specs=[in_hbm()] * 2,
            out_specs=[in_hbm()] * 3,
            scratch_shapes=[pltpu.VMEM((DONE * WIN, D), BF16)]
            + [pltpu.VMEM(*k) for k in kept]
            + [
                pltpu.VMEM((D, D), BF16),
                pltpu.SemaphoreType.DMA((DONE, MAXB)),
                pltpu.SemaphoreType.DMA,
                pltpu.SemaphoreType.DMA((DONE // OWN_GROUP, 3)),
            ],
        ),
        out_shape=[jax.ShapeDtypeStruct(*k) for k in kept],
        cost_estimate=pl.CostEstimate(
            flops=DONE * WIN * D * D * 64, bytes_accessed=DONE * WIN * D * 8, transcendentals=0
        ),
        name="own_head",
    )(starts, part, tokens, w_own)


def rows_of(tiles):
    return jnp.concatenate(
        [tiles[..., q, :, :].reshape(-1, HEAD) for q in range(N_MP)], axis=1
    )


def pack_kernel(
    start_ref, part_ref, core_ref, tokens_ref, w_ref, owner_ref, len_ref, off_ref,
    out_ref, rows_ref, x_s, table_s, row_s, out_s, sem, sem_t, sem_w, sem_out,
):
    tables = [
        pltpu.make_async_copy(ref, table_s.at[j], sem_t.at[j])
        for j, ref in enumerate((owner_ref, len_ref, off_ref))
    ]
    half = D // 2
    weights = pltpu.make_async_copy(w_ref.at[pl.ds(core_ref[0] * half, half)], rows_ref, sem_w)
    loads = [
        token_copies(
            tokens_ref, start_ref[0, part_ref[0] * MINE + k], x_s, k * WIN, sem.at[k]
        )
        for k in range(RAW)
    ]
    for copy in tables + loads[0] + [weights] + loads[1]:
        copy.start()
    row_s[...] = jnp.zeros_like(row_s)
    for j, copy in enumerate(tables):
        copy.wait()
        row_s[:, j * USERS : (j + 1) * USERS] = table_s[j]
    tile = jnp.broadcast_to(row_s[...], (TILE, 128)).astype(F32).astype(BF16)
    for k in range(RAW):
        out_s[k, :, N_MP] = jnp.broadcast_to(tile[None], (GROUPS, TILE, 128))
    sends = [pltpu.make_async_copy(out_s.at[k], out_ref.at[k], sem_out.at[k]) for k in range(RAW)]
    for k in range(RAW):
        for copy in loads[k]:
            copy.wait()
        for q in range(N_MP):
            out_s[k, :, q] = x_s[k * WIN : (k + 1) * WIN, q * HEAD : (q + 1) * HEAD].reshape(
                GROUPS, TILE, HEAD
            )
        sends[k].start()
    weights.wait()
    for copy in sends:
        copy.wait()


def pack(tokens, starts, part, core, w_own, owner, hist_len, recv_offset):
    shape = (RAW, GROUPS, RAW_MSG, TILE, HEAD)
    return pl.pallas_call(
        pack_kernel,
        grid_spec=pltpu.PrefetchScalarGridSpec(
            num_scalar_prefetch=3,
            grid=(1,),
            in_specs=[in_hbm()] * 5,
            out_specs=[in_hbm(), in_vmem()],
            scratch_shapes=[
                pltpu.VMEM((RAW * WIN, D), BF16),
                pltpu.VMEM((3, 1, USERS), jnp.int32),
                pltpu.VMEM((1, 128), jnp.int32),
                pltpu.VMEM(shape, BF16),
                pltpu.SemaphoreType.DMA((RAW, MAXB)),
                pltpu.SemaphoreType.DMA((3,)),
                pltpu.SemaphoreType.DMA,
                pltpu.SemaphoreType.DMA((RAW,)),
            ],
        ),
        out_shape=[jax.ShapeDtypeStruct(shape, BF16), pltpu.VMEM((D // 2, D), BF16)],
        name="pack",
    )(starts, part, core, tokens, w_own, owner, hist_len, recv_offset)


def head_order(part):
    return [part] + [(part + HEADS - s) % HEADS for s in range(1, HEADS)]


def mix(low_is_near, half_rows, first, near, far, w_out_of, x_rows):
    low = half_rows[:, : D // 2]
    high = half_rows[:, D // 2 :]
    parts = [jnp.where(low_is_near, low, high), jnp.where(low_is_near, high, low)]
    users = half_rows.shape[0] // WIN
    heads, gates = [first[0]], [first[1]]
    for near_ref, far_ref in zip(near, far):
        u, v, q, k = project(parts, [near_ref[...], far_ref[...]])
        gates.append(u)
        heads.append(attend_users(users, q, k, v))
    total = jnp.sum(heads[0] + heads[1] + (heads[2] + heads[3]), axis=1, keepdims=True)
    squares = jnp.sum(
        heads[0] * heads[0] + heads[1] * heads[1] + (heads[2] * heads[2] + heads[3] * heads[3]),
        axis=1,
        keepdims=True,
    )
    mean, inv = norm_stats(total, squares, 1.0 / WIN)
    gated = jnp.concatenate(
        [((a - mean) * inv * g.astype(F32)).astype(BF16) for a, g in zip(heads, gates)], axis=1
    )
    return jnp.dot(gated, w_out_of(), preferred_element_type=F32) + x_rows().astype(F32)


def attend_users(users, q, k, v):
    return jnp.concatenate(
        [attend(*(t[j * WIN : (j + 1) * WIN] for t in (q, k, v))) for j in range(users)], axis=0
    )


def live_rows(mixed, length):
    at = lax.broadcasted_iota(jnp.int32, (WIN, 1), 0)
    return jnp.where(at < length, mixed, 0.0).astype(BF16)


def last_row(tile, length):
    pick = lax.broadcasted_iota(jnp.int32, (TILE, HEAD), 0) == (length - 1) % TILE
    return jnp.sum(jnp.where(pick, tile.astype(F32), 0.0), axis=0, keepdims=True).astype(BF16)


def w_out_copies(part, w_out_ref, w_out_s, sem):
    return [
        pltpu.make_async_copy(
            w_out_ref.at[pl.ds(h * HEAD, HEAD)], w_out_s.at[pl.ds(s * HEAD, HEAD)], sem.at[s]
        )
        for s, h in enumerate(head_order(part))
    ]


def layer_kernel(
    start_ref, len_ref, part_ref, core_ref, tokens_ref, half_hbm, att_hbm, gate_hbm, *rest
):
    near, far = rest[: HEADS - 1], rest[HEADS - 1 : 2 * HEADS - 2]
    w_out_ref, out_ref, state_ref = rest[2 * HEADS - 2 : 2 * HEADS + 1]
    x_s, half_s, att_s, gate_s, w_out_s, out_s, sem_in, sem_w, sem_out = rest[2 * HEADS + 1 :]
    low_is_near = core_ref[0] == 0
    first_id = part_ref[0] * MINE + RAW

    def loads(i):
        rows = pl.ds(i * WIN, WIN)
        pairs = ((half_hbm, half_s), (att_hbm, att_s), (gate_hbm, gate_s))
        return [
            pltpu.make_async_copy(a.at[rows], b.at[rows], sem_in.at[i, MAXB + j])
            for j, (a, b) in enumerate(pairs)
        ] + token_copies(tokens_ref, start_ref[0, first_id + i], x_s, i * WIN, sem_in.at[i])

    weights = w_out_copies(part_ref[0], w_out_ref, w_out_s, sem_w)

    def sends(i):
        at = (i % HALVES, slice(None), pl.ds((i // HALVES) * N_MP, N_MP))
        return pltpu.make_async_copy(out_s.at[at], out_ref.at[at], sem_out.at[i])

    for i in range(DONE):
        for copy in loads(i):
            copy.start()
        if i == GROUP - 1:
            for copy in weights:
                copy.start()

    def group(step, carry):
        first_user = step * GROUP
        for j in range(GROUP):
            for copy in loads(first_user + j):
                copy.wait()
        rows = pl.ds(pl.multiple_of(first_user * WIN, WIN), GROUP * WIN)

        def w_out_of():
            @pl.when(step == 0)
            def _():
                for copy in weights:
                    copy.wait()

            return w_out_s[...]

        both = mix(
            low_is_near,
            half_s[rows, :],
            (att_s[rows, :], gate_s[rows, :]),
            near,
            far,
            w_out_of,
            lambda: x_s[rows, :],
        )
        for j in range(GROUP):
            i = first_user + j
            length = len_ref[0, first_id + i]
            half_id = i % HALVES
            base = (i // HALVES) * N_MP
            mixed = live_rows(both[j * WIN : (j + 1) * WIN], length)
            for q in range(N_MP):
                out_s[half_id, :, base + q] = mixed[:, q * HEAD : (q + 1) * HEAD].reshape(
                    GROUPS, TILE, HEAD
                )
            sends(i).start()
            for q in range(N_MP):
                state_ref[i, :, q * HEAD : (q + 1) * HEAD] = last_row(
                    out_s[half_id, (length - 1) // TILE, base + q], length
                )
        return carry

    lax.fori_loop(0, DONE // GROUP, group, 0)
    for i in range(DONE):
        sends(i).wait()


def layer(tokens, starts, lengths, part, core, kept, near, far, w_out):
    message = (HALVES, GROUPS, MSG, TILE, HEAD)
    return pl.pallas_call(
        layer_kernel,
        grid_spec=pltpu.PrefetchScalarGridSpec(
            num_scalar_prefetch=4,
            grid=(1,),
            in_specs=[in_hbm()] * 4 + [in_vmem()] * (2 * HEADS - 2) + [in_hbm()],
            out_specs=[in_hbm(), in_vmem()],
            scratch_shapes=[
                pltpu.VMEM((DONE * WIN, D), BF16),
                pltpu.VMEM((DONE * WIN, D), BF16),
                pltpu.VMEM((DONE * WIN, HEAD), F32),
                pltpu.VMEM((DONE * WIN, HEAD), BF16),
                pltpu.VMEM((D, D), BF16),
                pltpu.VMEM((HALVES, GROUPS, ROUND * N_MP, TILE, HEAD), BF16),
                pltpu.SemaphoreType.DMA((DONE, 5)),
                pltpu.SemaphoreType.DMA((HEADS,)),
                pltpu.SemaphoreType.DMA((DONE,)),
            ],
        ),
        out_shape=[
            jax.ShapeDtypeStruct(message, BF16),
            jax.ShapeDtypeStruct((DONE, 1, D), BF16),
        ],
        name="layer",
    )(starts, lengths, part, core, tokens, *kept, *map(keep, near), *map(keep, far), w_out)


def raw_kernel(first_tile, len_ref, part_ref, core_ref, src_ref, w_own_ref, *rest):
    near, far = rest[: HEADS - 1], rest[HEADS - 1 : 2 * HEADS - 2]
    w_out_ref = rest[2 * HEADS - 2]
    pieces = rest[2 * HEADS - 1 : 2 * HEADS - 1 + N_MP]
    state_ref, x_s, w_out_s, mixed_s, sem_x, sem_w = rest[2 * HEADS - 1 + N_MP :]
    part = part_ref[0]
    lengths = [len_ref[0, part * MINE + k] for k in range(RAW)]
    loads = [
        pltpu.make_async_copy(
            src_ref.at[pl.ds(k * GROUPS, GROUPS), pl.ds(first_tile, N_MP)], x_s.at[k], sem_x.at[k]
        )
        for k in range(RAW)
    ]
    weights = w_out_copies(part, w_out_ref, w_out_s, sem_w)
    for copy in loads + weights:
        copy.start()
    for copy in loads:
        copy.wait()

    def x_rows():
        return rows_of(x_s[...])

    half = norm_half(x_rows().astype(F32))
    u, v, q, k = project([half], [w_own_ref[...]])

    def w_out_of():
        for copy in weights:
            copy.wait()
        return w_out_s[...]

    both = mix(
        core_ref[0] == 0, half, (attend_users(RAW, q, k, v), u), near, far, w_out_of, x_rows
    )
    for k in range(RAW):
        mixed = live_rows(both[k * WIN : (k + 1) * WIN], lengths[k])
        for q in range(N_MP):
            mixed_s[q, k] = mixed[:, q * HEAD : (q + 1) * HEAD].reshape(GROUPS, TILE, HEAD)
        for q in range(N_MP):
            state_ref[k, :, q * HEAD : (q + 1) * HEAD] = last_row(
                mixed_s[q, k, (lengths[k] - 1) // TILE], lengths[k]
            )
    for s in range(N_MP):
        pieces[s][...] = mixed_s[(part + s) % N_MP]


def raw_layer(source, first_tile, lengths, part, core, w_own, near, far, w_out):
    piece = jax.ShapeDtypeStruct((RAW, GROUPS, TILE, HEAD), BF16)
    outs = pl.pallas_call(
        lambda *refs: raw_kernel(first_tile, *refs),
        grid_spec=pltpu.PrefetchScalarGridSpec(
            num_scalar_prefetch=3,
            grid=(1,),
            in_specs=[in_hbm()] + [in_vmem()] * (2 * HEADS - 1) + [in_hbm()],
            out_specs=[in_vmem()] * (N_MP + 1),
            scratch_shapes=[
                pltpu.VMEM((RAW, GROUPS, N_MP, TILE, HEAD), BF16),
                pltpu.VMEM((D, D), BF16),
                pltpu.VMEM((N_MP, RAW, GROUPS, TILE, HEAD), BF16),
                pltpu.SemaphoreType.DMA((RAW,)),
                pltpu.SemaphoreType.DMA((HEADS,)),
            ],
        ),
        out_shape=[piece] * N_MP + [jax.ShapeDtypeStruct((RAW, 1, D), BF16)],
    )(lengths, part, core, source, w_own, *near, *far, w_out)
    return outs[:N_MP], outs[N_MP]


def merge_kernel(first_ref, in_ref, msg_ref, out_ref, sorted_s, table_v, table_s, sem):
    table = jnp.max(in_ref[:, N_MP].astype(F32), axis=1)
    table_v[...] = table.astype(jnp.int32)
    copy = pltpu.make_async_copy(table_v, table_s, sem.at[0])
    copy.start()
    copy.wait()
    first = first_ref[0]

    def one(d, carry):
        o = table_s[d, first]
        for q in range(N_MP):
            sorted_s[o, q] = in_ref[d, q]
        return carry

    lax.fori_loop(0, N_DP, one, 0, unroll=8)
    send = pltpu.make_async_copy(sorted_s, out_ref.at[:, pl.ds(ROUND * N_MP, N_MP)], sem.at[1])
    send.start()
    send.wait()


def merge(spread, first, message):
    return pl.pallas_call(
        merge_kernel,
        grid_spec=pltpu.PrefetchScalarGridSpec(
            num_scalar_prefetch=1,
            grid=(1,),
            in_specs=[in_vmem(), in_hbm()],
            out_specs=in_hbm(),
            scratch_shapes=[
                pltpu.VMEM((N_DP, N_MP, TILE, HEAD), BF16),
                pltpu.VMEM((N_DP, 128), jnp.int32),
                pltpu.SMEM((N_DP, 128), jnp.int32),
                pltpu.SemaphoreType.DMA((2,)),
            ],
        ),
        out_shape=jax.ShapeDtypeStruct((N_DP, MSG, TILE, HEAD), BF16),
        input_output_aliases={2: 0},
        name="merge",
    )(first, keep(spread), message)


def regroup_kernel(from_ref, in_ref, out_ref, out_s, sem):
    chunk = N_DP // CHUNKS

    def send(c):
        at = pl.ds(c * chunk, chunk)
        return pltpu.make_async_copy(out_s.at[at], out_ref.at[at], sem.at[c])

    def one(c, carry):
        for j in range(chunk):
            o = c * chunk + j
            for r in range(ROUND):
                d = from_ref[r * N_DP + o]
                for q in range(N_MP):
                    out_s[o, q, r] = in_ref[d, r * N_MP + q]
        send(c).start()
        return carry

    lax.fori_loop(0, CHUNKS, one, 0)
    for c in range(CHUNKS):
        send(c).wait()


def regroup(spread, source):
    shape = (N_DP, N_MP, ROUND, TILE, HEAD)
    return pl.pallas_call(
        regroup_kernel,
        grid_spec=pltpu.PrefetchScalarGridSpec(
            num_scalar_prefetch=1,
            grid=(1,),
            in_specs=[in_vmem()],
            out_specs=in_hbm(),
            scratch_shapes=[pltpu.VMEM(shape, BF16), pltpu.SemaphoreType.DMA((CHUNKS,))],
        ),
        out_shape=jax.ShapeDtypeStruct(shape, BF16),
        name="regroup",
    )(source, keep(spread))


def place_kernel(len_ref, off_ref, part_ref, in_ref, own_ref, *rest):
    out_ref, zero_v, used_s, own_s, sem, sem_own = rest[N_MP - 1 :]
    pieces = (own_s, *rest[: N_MP - 1])
    load = pltpu.make_async_copy(own_ref, own_s, sem_own)
    load.start()
    per_block = BLOCK // TILE
    zero_v[...] = jnp.zeros_like(zero_v)

    def clear(b, carry):
        used_s[b] = 0
        return carry

    lax.fori_loop(0, BLK_DEV, clear, 0, unroll=8)

    def send(u, source):
        def block(j):
            to = off_ref[u] + j
            used_s[to] = 1
            pltpu.make_async_copy(
                source(pl.ds(j * per_block, per_block)),
                out_ref.at[pl.ds(to * per_block, per_block)],
                sem,
            ).start()

        block(0)

        @pl.when(len_ref[u] > BLOCK)
        def _():
            block(1)

    def send_piece(s):
        m = (part_ref[0] + N_MP - s) % N_MP
        for k in range(RAW):
            send(m * MINE + k, lambda rows: pieces[s].at[k, rows])

    for s in range(1, N_MP):
        send_piece(s)

    def one(n, carry):
        m = n // DONE
        i = n % DONE
        send(m * MINE + RAW + i, lambda rows: in_ref.at[i % HALVES, rows, m, i // HALVES])
        return carry

    lax.fori_loop(0, N_MP * DONE, one, 0)
    load.wait()
    send_piece(0)

    def fill(b, carry):
        @pl.when(used_s[b] == 0)
        def _():
            pltpu.make_async_copy(zero_v, out_ref.at[pl.ds(b * per_block, per_block)], sem).start()

        return carry

    lax.fori_loop(0, BLK_DEV, fill, 0)
    pltpu.make_async_copy(out_ref, out_ref, sem).wait()


def place(arrived, pieces, lengths, offsets, part):
    rows = BLK_DEV * BLOCK
    return pl.pallas_call(
        place_kernel,
        grid_spec=pltpu.PrefetchScalarGridSpec(
            num_scalar_prefetch=3,
            grid=(1,),
            in_specs=[in_vmem(), in_hbm()] + [in_vmem()] * (N_MP - 1),
            out_specs=in_hbm(),
            scratch_shapes=[
                pltpu.VMEM((BLOCK // TILE, TILE, HEAD), BF16),
                pltpu.SMEM((BLK_DEV,), jnp.int32),
                pltpu.VMEM((RAW, GROUPS, TILE, HEAD), BF16),
                pltpu.SemaphoreType.DMA,
                pltpu.SemaphoreType.DMA,
            ],
        ),
        out_shape=jax.ShapeDtypeStruct((rows // TILE, TILE, HEAD), BF16),
        compiler_params=pltpu.CompilerParams(vmem_limit_bytes=32 * 1024 * 1024),
        name="place",
    )(lengths, offsets, part, keep(arrived), pltpu.with_memory_space_constraint(pieces[0], pltpu.HBM), *map(keep, pieces[1:])).reshape(rows, HEAD)


def along_mp(array, s):
    return lax.ppermute(array, "mp", [(i, (i + s) % N_MP) for i in range(N_MP)])


def per_device(tokens, w_uvqk, w_out, hist_len, owner, recv_offset, block_start):
    me = lax.axis_index("dp")
    part = lax.axis_index("mp")
    first = part * MINE
    core = me % 2
    half = me // GROUPS
    part_1, core_1 = part[None], core[None]

    raw, mine_rows = pack(
        tokens, block_start, part_1, core_1, w_uvqk, owner, hist_len, recv_offset
    )
    near, far = [], []
    for s in range(1, N_MP):
        near.append(along_mp(mine_rows, s))
    for s in range(1, N_MP):
        far.append(lax.ppermute(near[s - 1], "dp", [(i, i ^ 1) for i in range(N_DP)]))

    raw_in = lax.all_to_all(
        raw.reshape(N_DP, RAW_MSG * TILE, HEAD), "dp", 0, 0, tiled=True
    ).reshape(N_DP, RAW_MSG, TILE, HEAD)
    kept = own_head(tokens, block_start, part_1, w_uvqk)
    message, last = layer(
        tokens, block_start, hist_len, part_1, core_1, kept, near, far, w_out
    )
    message = merge(
        raw_in, (first + half)[None], message.reshape(N_DP, MSG, TILE, HEAD)
    )
    spread = lax.all_to_all(
        message.reshape(N_DP, MSG * TILE, HEAD), "dp", 0, 0, tiled=True
    ).reshape(N_DP, MSG, TILE, HEAD)
    _, raw_last = raw_layer(
        raw.reshape(N_DP, RAW_MSG, TILE, HEAD), 0, hist_len, part_1, core_1,
        w_uvqk, near, far, w_out,
    )

    table = raw_in[:, N_MP, 0, :].astype(jnp.int32)
    owners = table[:, :USERS]
    held = lax.dynamic_slice_in_dim(owners, first + RAW + half, HALVES * (ROUND - 1) + 1, 1)
    ids = jnp.arange(N_DP, dtype=jnp.int32)
    source = jnp.sum(
        jnp.where(held[:, ::HALVES].T[:, None, :] == ids[None, :, None], ids[None, None, :], 0), axis=2
    ).reshape(-1)
    mine = owners == me
    recv_len = jnp.sum(jnp.where(mine, table[:, USERS : 2 * USERS], 0), axis=0)
    recv_off = jnp.sum(jnp.where(mine, table[:, 2 * USERS : 3 * USERS], 0), axis=0)

    sorted_rows = regroup(spread, source)
    arrived = lax.all_to_all(
        sorted_rows.reshape(N_DP * N_MP, ROUND * TILE, HEAD), ("dp", "mp"), 0, 0, tiled=True
    )
    pieces, _ = raw_layer(
        spread, ROUND * N_MP, recv_len[None], part_1, core_1,
        w_uvqk, near, far, w_out,
    )
    pieces = [pieces[0]] + [along_mp(pieces[s], s) for s in range(1, N_MP)]
    packed = place(
        arrived.reshape(HALVES, GROUPS, N_MP, ROUND, TILE, HEAD),
        pieces, recv_len, recv_off, part_1,
    )

    columns = jnp.concatenate([raw_last, last], axis=0).reshape(MINE, N_MP, HEAD)
    state = jnp.zeros((N_MP, MINE, HEAD), BF16)
    for s in range(N_MP):
        to_part = (part + s) % N_MP
        piece = lax.dynamic_slice_in_dim(columns, to_part, 1, 1)[:, 0]
        if s:
            piece = along_mp(piece, s)
        state = lax.dynamic_update_slice_in_dim(state, piece[None], (part - s) % N_MP, 0)
    return packed, state.reshape(USERS, HEAD)


def solution(mesh):
    in_specs = (
        P("dp", None),
        P(None, "mp"),
        P(),
        P("dp", None),
        P("dp", None),
        P("dp", None),
        P("dp", None),
    )
    out_specs = (P("dp", "mp"), P("dp", "mp"))
    return jax.shard_map(
        per_device, mesh=mesh, in_specs=in_specs, out_specs=out_specs, check_vma=False
    )
```

profile of v0, /device:TPU:1, one launch (start us, length us, event | category | flops | bytes accessed | tf_op | source)
XLA Modules:
  0.0 131.7 jit_solution(7800201532802921909)
XLA Ops:
  0.6 2.7 %pack.1 = (bf16[2,32,5,8,128]{4,3,2,1,0:T(8,128)(2,1)}, bf16[256,512]{1,0:T(8,128)(2,1)S(1)}) custom-call(s32[1,24]{1,0:T(1,128)} %start_ref.5, s32[1]{0:T(128)} %bitcast.part_ref.refs_1_, s32[1]{0:T(128)} %bitcast.1.core_ref.refs_2_, bf16[6144,512]{1,0:T(8,128)(2,1)} %tokens_ref.5, bf16[512,512]{1,0:T(8,128)(2,1)} %refs_4_.3, s32[1,24]{1,0:T(1,128)} %owner_ref.1, ...), custom_call_target="tpu_custom_call" | custom-call | tf_op jit(solution)/shard_map/pack/pallas_call | solution.py:228
  3.4 2.1 %collective-permute-start = (bf16[256,512]{1,0:T(8,128)(2,1)S(1)}, bf16[256,512]{1,0:T(8,128)(2,1)S(1)}, u32[]{:S(2)}, u32[]{:S(2)}) collective-permute-start(bf16[256,512]{1,0:T(8,128)(2,1)S(1)} %get-tuple-element.18), channel_id=1, source_target_pairs={{0,1},{1,2},{2,3},{3,0},{4,5},{5,6},{6,7},{7,4},{8,9},{9,10},{10,1... | collective-permute-start | bytes 786440 | tf_op jit(solution)/shard_map/ppermute | solution.py:637
  5.5 2.5 %collective-permute-start.1 = (bf16[256,512]{1,0:T(8,128)(2,1)S(1)}, bf16[256,512]{1,0:T(8,128)(2,1)S(1)}, u32[]{:S(2)}, u32[]{:S(2)}) collective-permute-start(bf16[256,512]{1,0:T(8,128)(2,1)S(1)} %get-tuple-element.18), channel_id=1, source_target_pairs={{0,2},{1,3},{2,0},{3,1},{4,6},{5,7},{6,4},{7,5},{8,10},{9,11},{10,... | collective-permute-start | bytes 786440 | tf_op jit(solution)/shard_map/ppermute | solution.py:637
  7.9 1.2 collective-permute-start.2
  9.1 13.2 %all-to-all-start = ((bf16[64,40,128]{2,1,0:T(8,128)(2,1)}), bf16[64,40,128]{2,1,0:T(8,128)(2,1)S(1)}, u32[]{:S(2)}, u32[]{:S(2)}) async-start(bf16[64,40,128]{2,1,0:T(8,128)(2,1)} %bitcast.41), calls=%async_computation | async-start | bytes 1310720 | tf_op jit(solution)/shard_map/all_to_all | solution.py:657
  22.3 0.0 collective-permute-done.rest_0_.refs_5_
  22.3 0.0 copy-start.2
  22.3 0.5 collective-permute-start.3
  22.8 0.0 collective-permute-done.1.rest_1_.refs_6_
  22.8 0.1 collective-permute-start.4
  23.0 0.0 collective-permute-done.2.rest_2_.refs_7_
  23.0 0.4 collective-permute-start.5
  23.4 5.0 %own_head.1 = (bf16[1024,512]{1,0:T(8,128)(2,1)}, f32[1024,128]{1,0:T(8,128)}, bf16[1024,128]{1,0:T(8,128)(2,1)}) custom-call(s32[1,24]{1,0:T(1,128)} %start_ref.5, s32[1]{0:T(128)} %bitcast.part_ref.refs_1_, bf16[6144,512]{1,0:T(8,128)(2,1)} %tokens_ref.5, bf16[512,512]{1,0:T(8,128)(2,1)} %refs_4_.3), custom_call_target="tpu_custom_call" | custom-call | flops 17179869184 | bytes 4194304 | tf_op jit(solution)/shard_map/own_head/pallas_call | solution.py:157
  28.4 0.0 collective-permute-done.3.rest_3_.refs_8_
  28.4 0.0 collective-permute-done.4.rest_4_.refs_9_
  28.4 0.0 collective-permute-done.5.rest_5_.refs_10_
  28.5 9.3 %layer.1 = (bf16[2,32,12,8,128]{4,3,2,1,0:T(8,128)(2,1)}, bf16[4,1,512]{2,1,0:T(2,128)(2,1)}) custom-call(s32[1,24]{1,0:T(1,128)} %start_ref.5, s32[1,24]{1,0:T(1,128)} %refs_0_.1, s32[1]{0:T(128)} %bitcast.part_ref.refs_1_, s32[1]{0:T(128)} %bitcast.1.core_ref.refs_2_, bf16[6144,512]{1,0:T(8,128)(2,1)} %tokens_ref.5, ...), custom_call_target="tpu_custom_call" | custom-call | tf_op jit(solution)/shard_map/layer/pallas_call | solution.py:381
  37.8 4.9 %all-to-all-done = bf16[64,40,128]{2,1,0:T(8,128)(2,1)S(1)} async-done(((bf16[64,40,128]{2,1,0:T(8,128)(2,1)}), bf16[64,40,128]{2,1,0:T(8,128)(2,1)S(1)}, u32[]{:S(2)}, u32[]{:S(2)}) %all-to-all-start) | async-done | bytes 655392 | tf_op jit(solution)/shard_map/all_to_all | solution.py:657
  42.6 2.1 %merge.1 = bf16[64,12,8,128]{3,2,1,0:T(8,128)(2,1)} custom-call(s32[1]{0:T(128)} %bitcast.6.first_ref, bf16[64,5,8,128]{3,2,1,0:T(8,128)(2,1)S(1)} %bitcast.35, bf16[64,12,8,128]{3,2,1,0:T(8,128)(2,1)} %bitcast.38), custom_call_target="tpu_custom_call", output_to_operand_aliasing={{}: (2, {})} | custom-call | tf_op jit(solution)/shard_map/merge/pallas_call | solution.py:496
  44.8 5.8 %all-to-all-start.1 = ((bf16[64,96,128]{2,1,0:T(8,128)(2,1)}), bf16[64,96,128]{2,1,0:T(8,128)(2,1)S(1)}, u32[]{:S(2)}, u32[]{:S(2)}) async-start(bf16[64,96,128]{2,1,0:T(8,128)(2,1)} %bitcast.39), calls=%async_computation.1 | async-start | bytes 3145728 | tf_op jit(solution)/shard_map/all_to_all | solution.py:667
  50.6 0.9 slice_convert_fusion
  51.5 0.6 fusion
  52.2 0.1 constant_dynamic-slice_fusion.4
  52.2 0.1 slice.19
  52.3 0.1 copy.12
  52.4 0.1 select_reduce_fusion
  52.5 0.6 reshape.45.from_ref
  53.1 36.5 %all-to-all-done.1 = bf16[64,96,128]{2,1,0:T(8,128)(2,1)S(1)} async-done(((bf16[64,96,128]{2,1,0:T(8,128)(2,1)}), bf16[64,96,128]{2,1,0:T(8,128)(2,1)S(1)}, u32[]{:S(2)}, u32[]{:S(2)}) %all-to-all-start.1) | async-done | bytes 1572896 | tf_op jit(solution)/shard_map/all_to_all | solution.py:667
  89.6 1.8 %regroup.1 = bf16[64,4,2,8,128]{4,3,2,1,0:T(8,128)(2,1)} custom-call(s32[128]{0:T(128)} %reshape.45.from_ref, bf16[64,12,8,128]{3,2,1,0:T(8,128)(2,1)S(1)} %bitcast.32), custom_call_target="tpu_custom_call" | custom-call | tf_op jit(solution)/shard_map/regroup/pallas_call | solution.py:540
  91.4 7.1 %all-to-all-start.2 = ((bf16[256,16,128]{2,1,0:T(8,128)(2,1)}), bf16[256,16,128]{2,1,0:T(8,128)(2,1)S(1)}, u32[]{:S(2)}, u32[]{:S(2)}) async-start(bf16[256,16,128]{2,1,0:T(8,128)(2,1)} %bitcast.40), calls=%async_computation.2 | async-start | bytes 2097152 | tf_op jit(solution)/shard_map/all_to_all | solution.py:687
  98.7 7.8 %shard_map.87 = (bf16[2,32,8,128]{3,2,1,0:T(8,128)(2,1)}, bf16[2,32,8,128]{3,2,1,0:T(8,128)(2,1)}, bf16[2,32,8,128]{3,2,1,0:T(8,128)(2,1)}, bf16[2,32,8,128]{3,2,1,0:T(8,128)(2,1)}, bf16[2,1,512]{2,1,0:T(2,128)(2,1)}) custom-call(s32[1,24]{1,0:T(1,128)} %refs_0_.1, s32[1]{0:T(128)} %bitcast.part_ref.refs_1_, s32[1]{0:T(128)} %bitcast.1.core_ref.refs_2_, ...), custom_call_target="tpu_custom_call" | custom-call | tf_op jit(solution)/shard_map/pallas_call | solution.py:455
  106.5 0.7 maximum_reduce_fusion
  107.3 1.4 %collective-permute-start.9 = (bf16[6,128]{1,0:T(8,128)(2,1)S(1)}, bf16[6,128]{1,0:T(8,128)(2,1)S(1)}, u32[]{:S(2)}, u32[]{:S(2)}) collective-permute-start(bf16[6,128]{1,0:T(8,128)(2,1)S(1)} %bitcast.48), channel_id=1, source_target_pairs={{0,1},{1,2},{2,3},{3,0},{4,5},{5,6},{6,7},{7,4},{8,9},{9,10},{10,1... | collective-permute-start | bytes 4616 | tf_op jit(solution)/shard_map/ppermute | solution.py:637
  108.7 2.4 %collective-permute-start.10 = (bf16[6,128]{1,0:T(8,128)(2,1)S(1)}, bf16[6,128]{1,0:T(8,128)(2,1)S(1)}, u32[]{:S(2)}, u32[]{:S(2)}) collective-permute-start(bf16[6,128]{1,0:T(8,128)(2,1)S(1)} %bitcast.47), channel_id=1, source_target_pairs={{0,2},{1,3},{2,0},{3,1},{4,6},{5,7},{6,4},{7,5},{8,10},{9,11},{10,... | collective-permute-start | bytes 4616 | tf_op jit(solution)/shard_map/ppermute | solution.py:637
  111.1 1.2 collective-permute-start.11
  112.3 0.0 collective-permute-done.9
  112.3 0.6 collective-permute-done.10
  113.0 7.9 %shard_map.86 = (bf16[2,32,8,128]{3,2,1,0:T(8,128)(2,1)}, bf16[2,32,8,128]{3,2,1,0:T(8,128)(2,1)}, bf16[2,32,8,128]{3,2,1,0:T(8,128)(2,1)}, bf16[2,32,8,128]{3,2,1,0:T(8,128)(2,1)}, bf16[2,1,512]{2,1,0:T(2,128)(2,1)}) custom-call(s32[1,24]{1,0:T(1,128)} %bitcast.37, s32[1]{0:T(128)} %bitcast.part_ref.refs_1_, s32[1]{0:T(128)} %bitcast.1.core_ref.refs_2_, ...), custom_call_target="tpu_custom_call" | custom-call | tf_op jit(solution)/shard_map/pallas_call | solution.py:455
  120.9 1.3 collective-permute-start.6
  122.2 1.3 %collective-permute-start.7 = (bf16[2,32,8,128]{3,2,1,0:T(8,128)(2,1)}, bf16[2,32,8,128]{3,2,1,0:T(8,128)(2,1)S(1)}, u32[]{:S(2)}, u32[]{:S(2)}) collective-permute-start(bf16[2,32,8,128]{3,2,1,0:T(8,128)(2,1)} %get-tuple-element.22), channel_id=1, source_target_pairs={{0,2},{1,3},{2,0},{3,1},{4,6},{5,7},{6,4},{7,5},{8,10},{9,11},{10,... | collective-permute-start | bytes 393224 | tf_op jit(solution)/shard_map/ppermute | solution.py:637
  123.5 2.0 %collective-permute-start.8 = (bf16[2,32,8,128]{3,2,1,0:T(8,128)(2,1)}, bf16[2,32,8,128]{3,2,1,0:T(8,128)(2,1)S(1)}, u32[]{:S(2)}, u32[]{:S(2)}) collective-permute-start(bf16[2,32,8,128]{3,2,1,0:T(8,128)(2,1)} %get-tuple-element.23), channel_id=1, source_target_pairs={{0,3},{1,0},{2,1},{3,2},{4,7},{5,4},{6,5},{7,6},{8,11},{9,8},{10,9... | collective-permute-start | bytes 393224 | tf_op jit(solution)/shard_map/ppermute | solution.py:637
  125.5 0.0 collective-permute-done.11
  125.5 0.6 reshape.54
  126.1 2.5 %collective-permute-done.6.rest_0_ = bf16[2,32,8,128]{3,2,1,0:T(8,128)(2,1)S(1)} collective-permute-done((bf16[2,32,8,128]{3,2,1,0:T(8,128)(2,1)}, bf16[2,32,8,128]{3,2,1,0:T(8,128)(2,1)S(1)}, u32[]{:S(2)}, u32[]{:S(2)}) %collective-permute-start.6) | collective-permute-done | bytes 131104 | tf_op jit(solution)/shard_map/ppermute | solution.py:637
  128.7 0.0 collective-permute-done.7.rest_1_
  128.7 0.1 collective-permute-done.8.rest_2_
  128.8 0.6 all-to-all-done.2
  129.4 2.1 %place.1 = bf16[768,8,128]{2,1,0:T(8,128)(2,1)} custom-call(s32[24]{0:T(128)S(1)} %copy-done.8, s32[24]{0:T(128)S(1)} %get-tuple-element.26.off_ref, s32[1]{0:T(128)} %bitcast.part_ref.refs_1_, bf16[2,32,4,2,8,128]{5,4,3,2,1,0:T(8,128)(2,1)S(1)} %bitcast.34, bf16[2,32,8,128]{3,2,1,0:T(8,128)(2,1)} %get-tuple-element.20.own_ref, ...), custom_call_target="tpu_custom_call" | custom-call | tf_op jit(solution)/shard_map/place/pallas_call | solution.py:615
  (29 shorter events, 0.1 us)
Async XLA Ops:
  3.4 18.9 %collective-permute-start = (bf16[256,512]{1,0:T(8,128)(2,1)S(1)}, bf16[256,512]{1,0:T(8,128)(2,1)S(1)}, u32[]{:S(2)}, u32[]{:S(2)}) collective-permute-start(bf16[256,512]{1,0:T(8,128)(2,1)S(1)} %get-tuple-element.18), channel_id=1, source_target_pairs={{0,1},{1,2},{2,3},{3,0},{4,5},{5,6},{6,7},{7,4},{8,9},{9,10},{10,1... | collective-permute-start | bytes 786440 | tf_op jit(solution)/shard_map/ppermute | solution.py:637
  5.5 17.3 %collective-permute-start.1 = (bf16[256,512]{1,0:T(8,128)(2,1)S(1)}, bf16[256,512]{1,0:T(8,128)(2,1)S(1)}, u32[]{:S(2)}, u32[]{:S(2)}) collective-permute-start(bf16[256,512]{1,0:T(8,128)(2,1)S(1)} %get-tuple-element.18), channel_id=1, source_target_pairs={{0,2},{1,3},{2,0},{3,1},{4,6},{5,7},{6,4},{7,5},{8,10},{9,11},{10,... | collective-permute-start | bytes 786440 | tf_op jit(solution)/shard_map/ppermute | solution.py:637
  7.9 15.0 %collective-permute-start.2 = (bf16[256,512]{1,0:T(8,128)(2,1)S(1)}, bf16[256,512]{1,0:T(8,128)(2,1)S(1)}, u32[]{:S(2)}, u32[]{:S(2)}) collective-permute-start(bf16[256,512]{1,0:T(8,128)(2,1)S(1)} %get-tuple-element.18), channel_id=1, source_target_pairs={{0,3},{1,0},{2,1},{3,2},{4,7},{5,4},{6,5},{7,6},{8,11},{9,8},{10,9... | collective-permute-start | bytes 786440 | tf_op jit(solution)/shard_map/ppermute | solution.py:637
  9.1 33.5 %all-to-all-start = ((bf16[64,40,128]{2,1,0:T(8,128)(2,1)}), bf16[64,40,128]{2,1,0:T(8,128)(2,1)S(1)}, u32[]{:S(2)}, u32[]{:S(2)}) async-start(bf16[64,40,128]{2,1,0:T(8,128)(2,1)} %bitcast.41), calls=%async_computation | async-start | bytes 1310720 | tf_op jit(solution)/shard_map/all_to_all | solution.py:657
  22.3 6.2 %copy-start.2 = (bf16[256,512]{1,0:T(8,128)(2,1)}, bf16[256,512]{1,0:T(8,128)(2,1)S(1)}, u32[]{:S(2)}) copy-start(bf16[256,512]{1,0:T(8,128)(2,1)S(1)} %collective-permute-done.rest_0_.refs_5_) | copy-start | bytes 786436
  22.3 6.1 %collective-permute-start.3 = (bf16[256,512]{1,0:T(8,128)(2,1)S(1)}, bf16[256,512]{1,0:T(8,128)(2,1)S(1)}, u32[]{:S(2)}, u32[]{:S(2)}) collective-permute-start(bf16[256,512]{1,0:T(8,128)(2,1)S(1)} %collective-permute-done.rest_0_.refs_5_), channel_id=1, source_target_pairs={{0,4},{4,0},{8,12},{12,8},{16,20},{20,16},{24,28},{28,24},{32,36},... | collective-permute-start | bytes 786440 | tf_op jit(solution)/shard_map/ppermute | solution.py:655
  22.8 5.6 %copy-start.3 = (bf16[256,512]{1,0:T(8,128)(2,1)}, bf16[256,512]{1,0:T(8,128)(2,1)S(1)}, u32[]{:S(2)}) copy-start(bf16[256,512]{1,0:T(8,128)(2,1)S(1)} %collective-permute-done.1.rest_1_.refs_6_) | copy-start | bytes 786436
  22.8 5.6 %collective-permute-start.4 = (bf16[256,512]{1,0:T(8,128)(2,1)S(1)}, bf16[256,512]{1,0:T(8,128)(2,1)S(1)}, u32[]{:S(2)}, u32[]{:S(2)}) collective-permute-start(bf16[256,512]{1,0:T(8,128)(2,1)S(1)} %collective-permute-done.1.rest_1_.refs_6_), channel_id=1, source_target_pairs={{0,4},{4,0},{8,12},{12,8},{16,20},{20,16},{24,28},{28,24},{32,36},... | collective-permute-start | bytes 786440 | tf_op jit(solution)/shard_map/ppermute | solution.py:655
  23.0 5.5 %copy-start.4 = (bf16[256,512]{1,0:T(8,128)(2,1)}, bf16[256,512]{1,0:T(8,128)(2,1)S(1)}, u32[]{:S(2)}) copy-start(bf16[256,512]{1,0:T(8,128)(2,1)S(1)} %collective-permute-done.2.rest_2_.refs_7_) | copy-start | bytes 786436
  23.0 5.5 %collective-permute-start.5 = (bf16[256,512]{1,0:T(8,128)(2,1)S(1)}, bf16[256,512]{1,0:T(8,128)(2,1)S(1)}, u32[]{:S(2)}, u32[]{:S(2)}) collective-permute-start(bf16[256,512]{1,0:T(8,128)(2,1)S(1)} %collective-permute-done.2.rest_2_.refs_7_), channel_id=1, source_target_pairs={{0,4},{4,0},{8,12},{12,8},{16,20},{20,16},{24,28},{28,24},{32,36},... | collective-permute-start | bytes 786440 | tf_op jit(solution)/shard_map/ppermute | solution.py:655
  28.4 9.3 %copy-start.5 = (bf16[256,512]{1,0:T(8,128)(2,1)}, bf16[256,512]{1,0:T(8,128)(2,1)S(1)}, u32[]{:S(2)}) copy-start(bf16[256,512]{1,0:T(8,128)(2,1)S(1)} %collective-permute-done.3.rest_3_.refs_8_) | copy-start | bytes 786436
  28.4 9.3 %copy-start.6 = (bf16[256,512]{1,0:T(8,128)(2,1)}, bf16[256,512]{1,0:T(8,128)(2,1)S(1)}, u32[]{:S(2)}) copy-start(bf16[256,512]{1,0:T(8,128)(2,1)S(1)} %collective-permute-done.4.rest_4_.refs_9_) | copy-start | bytes 786436
  28.4 9.3 %copy-start.7 = (bf16[256,512]{1,0:T(8,128)(2,1)}, bf16[256,512]{1,0:T(8,128)(2,1)S(1)}, u32[]{:S(2)}) copy-start(bf16[256,512]{1,0:T(8,128)(2,1)S(1)} %collective-permute-done.5.rest_5_.refs_10_) | copy-start | bytes 786436
  42.6 2.1 %copy-start.1 = (bf16[64,40,128]{2,1,0:T(8,128)(2,1)}, bf16[64,40,128]{2,1,0:T(8,128)(2,1)S(1)}, u32[]{:S(2)}) copy-start(bf16[64,40,128]{2,1,0:T(8,128)(2,1)S(1)} %all-to-all-done) | copy-start | bytes 1966084
  44.8 44.9 %all-to-all-start.1 = ((bf16[64,96,128]{2,1,0:T(8,128)(2,1)}), bf16[64,96,128]{2,1,0:T(8,128)(2,1)S(1)}, u32[]{:S(2)}, u32[]{:S(2)}) async-start(bf16[64,96,128]{2,1,0:T(8,128)(2,1)} %bitcast.39), calls=%async_computation.1 | async-start | bytes 3145728 | tf_op jit(solution)/shard_map/all_to_all | solution.py:667
  89.6 1.8 %copy-start = (bf16[64,96,128]{2,1,0:T(8,128)(2,1)}, bf16[64,96,128]{2,1,0:T(8,128)(2,1)S(1)}, u32[]{:S(2)}) copy-start(bf16[64,96,128]{2,1,0:T(8,128)(2,1)S(1)} %all-to-all-done.1) | copy-start | bytes 4718596
  91.4 38.0 %all-to-all-start.2 = ((bf16[256,16,128]{2,1,0:T(8,128)(2,1)}), bf16[256,16,128]{2,1,0:T(8,128)(2,1)S(1)}, u32[]{:S(2)}, u32[]{:S(2)}) async-start(bf16[256,16,128]{2,1,0:T(8,128)(2,1)} %bitcast.40), calls=%async_computation.2 | async-start | bytes 2097152 | tf_op jit(solution)/shard_map/all_to_all | solution.py:687
  98.7 7.8 %copy-start.9 = (bf16[4,1,512]{2,1,0:T(2,128)(2,1)S(1)}, bf16[4,1,512]{2,1,0:T(2,128)(2,1)}, u32[]{:S(2)}) copy-start(bf16[4,1,512]{2,1,0:T(2,128)(2,1)} %get-tuple-element.25) | copy-start | bytes 12292
  107.3 5.0 %collective-permute-start.9 = (bf16[6,128]{1,0:T(8,128)(2,1)S(1)}, bf16[6,128]{1,0:T(8,128)(2,1)S(1)}, u32[]{:S(2)}, u32[]{:S(2)}) collective-permute-start(bf16[6,128]{1,0:T(8,128)(2,1)S(1)} %bitcast.48), channel_id=1, source_target_pairs={{0,1},{1,2},{2,3},{3,0},{4,5},{5,6},{6,7},{7,4},{8,9},{9,10},{10,1... | collective-permute-start | bytes 4616 | tf_op jit(solution)/shard_map/ppermute | solution.py:637
  108.7 4.2 %collective-permute-start.10 = (bf16[6,128]{1,0:T(8,128)(2,1)S(1)}, bf16[6,128]{1,0:T(8,128)(2,1)S(1)}, u32[]{:S(2)}, u32[]{:S(2)}) collective-permute-start(bf16[6,128]{1,0:T(8,128)(2,1)S(1)} %bitcast.47), channel_id=1, source_target_pairs={{0,2},{1,3},{2,0},{3,1},{4,6},{5,7},{6,4},{7,5},{8,10},{9,11},{10,... | collective-permute-start | bytes 4616 | tf_op jit(solution)/shard_map/ppermute | solution.py:637
  111.1 14.4 %collective-permute-start.11 = (bf16[6,128]{1,0:T(8,128)(2,1)S(1)}, bf16[6,128]{1,0:T(8,128)(2,1)S(1)}, u32[]{:S(2)}, u32[]{:S(2)}) collective-permute-start(bf16[6,128]{1,0:T(8,128)(2,1)S(1)} %bitcast.46), channel_id=1, source_target_pairs={{0,3},{1,0},{2,1},{3,2},{4,7},{5,4},{6,5},{7,6},{8,11},{9,8},{10,9... | collective-permute-start | bytes 4616 | tf_op jit(solution)/shard_map/ppermute | solution.py:637
  113.0 16.5 %copy-start.8 = (s32[24]{0:T(128)S(1)}, s32[24]{0:T(128)}, u32[]{:S(2)}) copy-start(s32[24]{0:T(128)} %get-tuple-element.27.len_ref) | copy-start | bytes 292
  120.9 7.8 %collective-permute-start.6 = (bf16[2,32,8,128]{3,2,1,0:T(8,128)(2,1)}, bf16[2,32,8,128]{3,2,1,0:T(8,128)(2,1)S(1)}, u32[]{:S(2)}, u32[]{:S(2)}) collective-permute-start(bf16[2,32,8,128]{3,2,1,0:T(8,128)(2,1)} %get-tuple-element.21), channel_id=1, source_target_pairs={{0,1},{1,2},{2,3},{3,0},{4,5},{5,6},{6,7},{7,4},{8,9},{9,10},{10,1... | collective-permute-start | bytes 393224 | tf_op jit(solution)/shard_map/ppermute | solution.py:637
  122.2 6.5 %collective-permute-start.7 = (bf16[2,32,8,128]{3,2,1,0:T(8,128)(2,1)}, bf16[2,32,8,128]{3,2,1,0:T(8,128)(2,1)S(1)}, u32[]{:S(2)}, u32[]{:S(2)}) collective-permute-start(bf16[2,32,8,128]{3,2,1,0:T(8,128)(2,1)} %get-tuple-element.22), channel_id=1, source_target_pairs={{0,2},{1,3},{2,0},{3,1},{4,6},{5,7},{6,4},{7,5},{8,10},{9,11},{10,... | collective-permute-start | bytes 393224 | tf_op jit(solution)/shard_map/ppermute | solution.py:637
  123.5 5.3 %collective-permute-start.8 = (bf16[2,32,8,128]{3,2,1,0:T(8,128)(2,1)}, bf16[2,32,8,128]{3,2,1,0:T(8,128)(2,1)S(1)}, u32[]{:S(2)}, u32[]{:S(2)}) collective-permute-start(bf16[2,32,8,128]{3,2,1,0:T(8,128)(2,1)} %get-tuple-element.23), channel_id=1, source_target_pairs={{0,3},{1,0},{2,1},{3,2},{4,7},{5,4},{6,5},{7,6},{8,11},{9,8},{10,9... | collective-permute-start | bytes 393224 | tf_op jit(solution)/shard_map/ppermute | solution.py:637
where the time goes:
time: 134 us; the launch traced here: 132 us
  waiting for transfers between devices  45.3 us (34%)
  starting transfers between devices  42.5 us (32%)
  Pallas kernels  38.7 us (29%)
  other arithmetic  2.41 us (2%)
  local copies, waits for them, and re-layouts  1.57 us (1%)
    all_to_all x1, waiting for transfers between devices, per_device(): lax.all_to_all(message.reshape(N_DP, MSG * TILE, HEAD), 'dp', 0, 0, tiled...  36.5 us
    pallas_call x2, Pallas kernels, raw_layer(): pl.pallas_call(lambda *refs: raw_kernel(first_tile, *refs), grid_spec=plt...  15.7 us
    ppermute x9, starting transfers between devices, along_mp(): return lax.ppermute(array, 'mp', [(i, (i + s) % N_MP) for i in range(N_MP)])  15.3 us
    all_to_all x1, starting transfers between devices, per_device(): lax.all_to_all(raw.reshape(N_DP, RAW_MSG * TILE, HEAD), 'dp', 0, 0, tiled...  13.2 us
    pallas_call x1, Pallas kernels, layer(): pl.pallas_call(layer_kernel, grid_spec=pltpu.PrefetchScalarGridSpec(num_s...  9.25 us
    all_to_all x1, starting transfers between devices, per_device(): lax.all_to_all(sorted_rows.reshape(N_DP * N_MP, ROUND * TILE, HEAD), ('dp...  7.13 us
    all_to_all x1, starting transfers between devices, per_device(): lax.all_to_all(message.reshape(N_DP, MSG * TILE, HEAD), 'dp', 0, 0, tiled...  5.81 us
    pallas_call x1, Pallas kernels, own_head(): pl.pallas_call(own_head_kernel, grid_spec=pltpu.PrefetchScalarGridSpec(nu...  5 us
  transfers between devices with their start and end apart: 15, of which 6 were waited for; matrix products, arithmetic and copies ran while one was open for 3% of the time, Pallas kernels for 23%

commit v1 on v0

--- a/solution.py
+++ b/solution.py
@@ -24,6 +24,7 @@
 GROUP = 2
 OWN_GROUP = 2
 CHUNKS = 4
+SEATS = list(range(N_DP - 1, -1, -1))
 RAW_MSG = N_MP + 1
 ROUND = DONE // HALVES
 MSG = (ROUND + 1) * N_MP
@@ -205,7 +206,7 @@
     row_s[...] = jnp.zeros_like(row_s)
     for j, copy in enumerate(tables):
         copy.wait()
-        row_s[:, j * USERS : (j + 1) * USERS] = table_s[j]
+        row_s[:, j * USERS : (j + 1) * USERS] = table_s[j] if j else N_DP - 1 - table_s[j]
     tile = jnp.broadcast_to(row_s[...], (TILE, 128)).astype(F32).astype(BF16)
     for k in range(RAW):
         out_s[k, :, N_MP] = jnp.broadcast_to(tile[None], (GROUPS, TILE, 128))
@@ -642,7 +643,8 @@
     part = lax.axis_index("mp")
     first = part * MINE
     core = me % 2
-    half = me // GROUPS
+    seat = N_DP - 1 - me
+    half = seat // GROUPS
     part_1, core_1 = part[None], core[None]
 
     raw, mine_rows = pack(
@@ -655,7 +657,7 @@
         far.append(lax.ppermute(near[s - 1], "dp", [(i, i ^ 1) for i in range(N_DP)]))
 
     raw_in = lax.all_to_all(
-        raw.reshape(N_DP, RAW_MSG * TILE, HEAD), "dp", 0, 0, tiled=True
+        raw.reshape(N_DP, RAW_MSG * TILE, HEAD), "dp", 0, 0, axis_index_groups=[SEATS], tiled=True
     ).reshape(N_DP, RAW_MSG, TILE, HEAD)
     kept = own_head(tokens, block_start, part_1, w_uvqk)
     message, last = layer(
@@ -665,7 +667,7 @@
         raw_in, (first + half)[None], message.reshape(N_DP, MSG, TILE, HEAD)
     )
     spread = lax.all_to_all(
-        message.reshape(N_DP, MSG * TILE, HEAD), "dp", 0, 0, tiled=True
+        message.reshape(N_DP, MSG * TILE, HEAD), "dp", 0, 0, axis_index_groups=[SEATS], tiled=True
     ).reshape(N_DP, MSG, TILE, HEAD)
     _, raw_last = raw_layer(
         raw.reshape(N_DP, RAW_MSG, TILE, HEAD), 0, hist_len, part_1, core_1,
@@ -679,13 +681,14 @@
     source = jnp.sum(
         jnp.where(held[:, ::HALVES].T[:, None, :] == ids[None, :, None], ids[None, None, :], 0), axis=2
     ).reshape(-1)
-    mine = owners == me
+    mine = owners == seat
     recv_len = jnp.sum(jnp.where(mine, table[:, USERS : 2 * USERS], 0), axis=0)
     recv_off = jnp.sum(jnp.where(mine, table[:, 2 * USERS : 3 * USERS], 0), axis=0)
 
     sorted_rows = regroup(spread, source)
     arrived = lax.all_to_all(
-        sorted_rows.reshape(N_DP * N_MP, ROUND * TILE, HEAD), ("dp", "mp"), 0, 0, tiled=True
+        sorted_rows.reshape(N_DP * N_MP, ROUND * TILE, HEAD), ("dp", "mp"), 0, 0,
+        axis_index_groups=[[d * N_MP + m for d in SEATS for m in range(N_MP)]], tiled=True
     )
     pieces, _ = raw_layer(
         spread, ROUND * N_MP, recv_len[None], part_1, core_1,

time: 134 us -> 134 us (level)
  starting transfers between devices: 42.5 us -> 49.6 us
  waiting for transfers between devices: 45.3 us -> 38.6 us
    all_to_all x2, waiting for transfers between devices: 41.4 us -> 34.5 us  [the longest x1 33.4 us: per_device(): lax.all_to_all(message.reshape(N_DP, MSG * TILE, HEAD), 'dp', 0, 0, axis_...]
    all_to_all x2, starting transfers between devices: 19 us -> 23.2 us  [the longest x1 13.9 us: per_device(): lax.all_to_all(raw.reshape(N_DP, RAW_MSG * TILE, HEAD), 'dp', 0, 0, axis_...]
    all_to_all x1, starting transfers between devices: 7.13 us -> 10.2 us  [per_device(): lax.all_to_all(sorted_rows.reshape(N_DP * N_MP, ROUND * TILE, HEAD), ('dp...]
where the time goes in v1:
time: 134 us; the launch traced here: 132 us
  starting transfers between devices  49.6 us (37%)
  Pallas kernels  38.7 us (29%)
  waiting for transfers between devices  38.6 us (29%)
  other arithmetic  2.41 us (2%)
  local copies, waits for them, and re-layouts  1.57 us (1%)
    all_to_all x1, waiting for transfers between devices, per_device(): lax.all_to_all(message.reshape(N_DP, MSG * TILE, HEAD), 'dp', 0, 0, axis_...  33.4 us
    pallas_call x2, Pallas kernels, raw_layer(): pl.pallas_call(lambda *refs: raw_kernel(first_tile, *refs), grid_spec=plt...  15.7 us
    ppermute x9, starting transfers between devices, along_mp(): return lax.ppermute(array, 'mp', [(i, (i + s) % N_MP) for i in range(N_MP)])  15.3 us
    all_to_all x1, starting transfers between devices, per_device(): lax.all_to_all(raw.reshape(N_DP, RAW_MSG * TILE, HEAD), 'dp', 0, 0, axis_...  13.9 us
    all_to_all x1, starting transfers between devices, per_device(): lax.all_to_all(sorted_rows.reshape(N_DP * N_MP, ROUND * TILE, HEAD), ('dp...  10.2 us
    all_to_all x1, starting transfers between devices, per_device(): lax.all_to_all(message.reshape(N_DP, MSG * TILE, HEAD), 'dp', 0, 0, axis_...  9.34 us
    pallas_call x1, Pallas kernels, layer(): pl.pallas_call(layer_kernel, grid_spec=pltpu.PrefetchScalarGridSpec(num_s...  9.25 us
    pallas_call x1, Pallas kernels, own_head(): pl.pallas_call(own_head_kernel, grid_spec=pltpu.PrefetchScalarGridSpec(nu...  5 us
  transfers between devices with their start and end apart: 15, of which 6 were waited for; matrix products, arithmetic and copies ran while one was open for 3% of the time, Pallas kernels for 23%

profile of v1, /device:TPU:1, one launch (start us, length us, event | category | flops | bytes accessed | tf_op | source)
XLA Modules:
  0.0 132.1 jit_solution(8570500129462048475)
XLA Ops:
  0.6 2.7 %pack.1 = (bf16[2,32,5,8,128]{4,3,2,1,0:T(8,128)(2,1)}, bf16[256,512]{1,0:T(8,128)(2,1)S(1)}) custom-call(s32[1,24]{1,0:T(1,128)} %start_ref.5, s32[1]{0:T(128)} %bitcast.part_ref.refs_1_, s32[1]{0:T(128)} %bitcast.1.core_ref.refs_2_, bf16[6144,512]{1,0:T(8,128)(2,1)} %tokens_ref.5, bf16[512,512]{1,0:T(8,128)(2,1)} %refs_4_.3, s32[1,24]{1,0:T(1,128)} %owner_ref.1, ...), custom_call_target="tpu_custom_call" | custom-call | tf_op jit(solution)/shard_map/pack/pallas_call | solution.py:229
  3.4 2.1 %collective-permute-start = (bf16[256,512]{1,0:T(8,128)(2,1)S(1)}, bf16[256,512]{1,0:T(8,128)(2,1)S(1)}, u32[]{:S(2)}, u32[]{:S(2)}) collective-permute-start(bf16[256,512]{1,0:T(8,128)(2,1)S(1)} %get-tuple-element.18), channel_id=1, source_target_pairs={{0,1},{1,2},{2,3},{3,0},{4,5},{5,6},{6,7},{7,4},{8,9},{9,10},{10,1... | collective-permute-start | bytes 786440 | tf_op jit(solution)/shard_map/ppermute | solution.py:638
  5.5 2.5 %collective-permute-start.1 = (bf16[256,512]{1,0:T(8,128)(2,1)S(1)}, bf16[256,512]{1,0:T(8,128)(2,1)S(1)}, u32[]{:S(2)}, u32[]{:S(2)}) collective-permute-start(bf16[256,512]{1,0:T(8,128)(2,1)S(1)} %get-tuple-element.18), channel_id=1, source_target_pairs={{0,2},{1,3},{2,0},{3,1},{4,6},{5,7},{6,4},{7,5},{8,10},{9,11},{10,... | collective-permute-start | bytes 786440 | tf_op jit(solution)/shard_map/ppermute | solution.py:638
  7.9 1.2 collective-permute-start.2
  9.1 13.9 %all-to-all-start = ((bf16[64,40,128]{2,1,0:T(8,128)(2,1)}), bf16[64,40,128]{2,1,0:T(8,128)(2,1)S(1)}, u32[]{:S(2)}, u32[]{:S(2)}) async-start(bf16[64,40,128]{2,1,0:T(8,128)(2,1)} %bitcast.41), calls=%async_computation | async-start | bytes 1310720 | tf_op jit(solution)/shard_map/all_to_all | solution.py:659
  23.0 0.0 collective-permute-done.rest_0_.refs_5_
  23.0 0.5 collective-permute-start.3
  23.5 0.0 collective-permute-done.1.rest_1_.refs_6_
  23.5 0.1 collective-permute-start.4
  23.6 0.0 collective-permute-done.2.rest_2_.refs_7_
  23.6 0.4 collective-permute-start.5
  24.0 5.0 %own_head.1 = (bf16[1024,512]{1,0:T(8,128)(2,1)}, f32[1024,128]{1,0:T(8,128)}, bf16[1024,128]{1,0:T(8,128)(2,1)}) custom-call(s32[1,24]{1,0:T(1,128)} %start_ref.5, s32[1]{0:T(128)} %bitcast.part_ref.refs_1_, bf16[6144,512]{1,0:T(8,128)(2,1)} %tokens_ref.5, bf16[512,512]{1,0:T(8,128)(2,1)} %refs_4_.3), custom_call_target="tpu_custom_call" | custom-call | flops 17179869184 | bytes 4194304 | tf_op jit(solution)/shard_map/own_head/pallas_call | solution.py:158
  29.0 0.0 collective-permute-done.3.rest_3_.refs_8_
  29.0 0.0 collective-permute-done.4.rest_4_.refs_9_
  29.0 0.0 copy-start.6
  29.1 0.0 collective-permute-done.5.rest_5_.refs_10_
  29.1 9.3 %layer.1 = (bf16[2,32,12,8,128]{4,3,2,1,0:T(8,128)(2,1)}, bf16[4,1,512]{2,1,0:T(2,128)(2,1)}) custom-call(s32[1,24]{1,0:T(1,128)} %start_ref.5, s32[1,24]{1,0:T(1,128)} %refs_0_.1, s32[1]{0:T(128)} %bitcast.part_ref.refs_1_, s32[1]{0:T(128)} %bitcast.1.core_ref.refs_2_, bf16[6144,512]{1,0:T(8,128)(2,1)} %tokens_ref.5, ...), custom_call_target="tpu_custom_call" | custom-call | tf_op jit(solution)/shard_map/layer/pallas_call | solution.py:382
  38.4 1.1 all-to-all-done
  39.5 2.1 %merge.1 = bf16[64,12,8,128]{3,2,1,0:T(8,128)(2,1)} custom-call(s32[1]{0:T(128)} %bitcast.6.first_ref, bf16[64,5,8,128]{3,2,1,0:T(8,128)(2,1)S(1)} %bitcast.35, bf16[64,12,8,128]{3,2,1,0:T(8,128)(2,1)} %bitcast.38), custom_call_target="tpu_custom_call", output_to_operand_aliasing={{}: (2, {})} | custom-call | tf_op jit(solution)/shard_map/merge/pallas_call | solution.py:497
  41.6 9.3 %all-to-all-start.1 = ((bf16[64,96,128]{2,1,0:T(8,128)(2,1)}), bf16[64,96,128]{2,1,0:T(8,128)(2,1)S(1)}, u32[]{:S(2)}, u32[]{:S(2)}) async-start(bf16[64,96,128]{2,1,0:T(8,128)(2,1)} %bitcast.39), calls=%async_computation.1 | async-start | bytes 3145728 | tf_op jit(solution)/shard_map/all_to_all | solution.py:669
  51.0 0.9 slice_convert_fusion
  51.9 0.6 fusion
  52.6 0.1 constant_dynamic-slice_fusion.4
  52.6 0.1 slice.19
  52.7 0.1 copy.12
  52.8 0.1 select_reduce_fusion
  52.9 0.6 reshape.45.from_ref
  53.5 33.4 %all-to-all-done.1 = bf16[64,96,128]{2,1,0:T(8,128)(2,1)S(1)} async-done(((bf16[64,96,128]{2,1,0:T(8,128)(2,1)}), bf16[64,96,128]{2,1,0:T(8,128)(2,1)S(1)}, u32[]{:S(2)}, u32[]{:S(2)}) %all-to-all-start.1) | async-done | bytes 1572896 | tf_op jit(solution)/shard_map/all_to_all | solution.py:669
  86.9 1.8 %regroup.1 = bf16[64,4,2,8,128]{4,3,2,1,0:T(8,128)(2,1)} custom-call(s32[128]{0:T(128)} %reshape.45.from_ref, bf16[64,12,8,128]{3,2,1,0:T(8,128)(2,1)S(1)} %bitcast.32), custom_call_target="tpu_custom_call" | custom-call | tf_op jit(solution)/shard_map/regroup/pallas_call | solution.py:541
  88.7 10.2 %all-to-all-start.2 = ((bf16[256,16,128]{2,1,0:T(8,128)(2,1)}), bf16[256,16,128]{2,1,0:T(8,128)(2,1)S(1)}, u32[]{:S(2)}, u32[]{:S(2)}) async-start(bf16[256,16,128]{2,1,0:T(8,128)(2,1)} %bitcast.40), calls=%async_computation.2 | async-start | bytes 2097152 | tf_op jit(solution)/shard_map/all_to_all | solution.py:689
  99.0 7.8 %shard_map.87 = (bf16[2,32,8,128]{3,2,1,0:T(8,128)(2,1)}, bf16[2,32,8,128]{3,2,1,0:T(8,128)(2,1)}, bf16[2,32,8,128]{3,2,1,0:T(8,128)(2,1)}, bf16[2,32,8,128]{3,2,1,0:T(8,128)(2,1)}, bf16[2,1,512]{2,1,0:T(2,128)(2,1)}) custom-call(s32[1,24]{1,0:T(1,128)} %refs_0_.1, s32[1]{0:T(128)} %bitcast.part_ref.refs_1_, s32[1]{0:T(128)} %bitcast.1.core_ref.refs_2_, ...), custom_call_target="tpu_custom_call" | custom-call | tf_op jit(solution)/shard_map/pallas_call | solution.py:456
  106.8 0.7 maximum_reduce_fusion
  107.6 1.4 %collective-permute-start.9 = (bf16[6,128]{1,0:T(8,128)(2,1)S(1)}, bf16[6,128]{1,0:T(8,128)(2,1)S(1)}, u32[]{:S(2)}, u32[]{:S(2)}) collective-permute-start(bf16[6,128]{1,0:T(8,128)(2,1)S(1)} %bitcast.48), channel_id=1, source_target_pairs={{0,1},{1,2},{2,3},{3,0},{4,5},{5,6},{6,7},{7,4},{8,9},{9,10},{10,1... | collective-permute-start | bytes 4616 | tf_op jit(solution)/shard_map/ppermute | solution.py:638
  109.0 2.4 %collective-permute-start.10 = (bf16[6,128]{1,0:T(8,128)(2,1)S(1)}, bf16[6,128]{1,0:T(8,128)(2,1)S(1)}, u32[]{:S(2)}, u32[]{:S(2)}) collective-permute-start(bf16[6,128]{1,0:T(8,128)(2,1)S(1)} %bitcast.47), channel_id=1, source_target_pairs={{0,2},{1,3},{2,0},{3,1},{4,6},{5,7},{6,4},{7,5},{8,10},{9,11},{10,... | collective-permute-start | bytes 4616 | tf_op jit(solution)/shard_map/ppermute | solution.py:638
  111.4 1.2 collective-permute-start.11
  112.6 0.0 collective-permute-done.9
  112.6 0.6 collective-permute-done.10
  113.3 7.9 %shard_map.86 = (bf16[2,32,8,128]{3,2,1,0:T(8,128)(2,1)}, bf16[2,32,8,128]{3,2,1,0:T(8,128)(2,1)}, bf16[2,32,8,128]{3,2,1,0:T(8,128)(2,1)}, bf16[2,32,8,128]{3,2,1,0:T(8,128)(2,1)}, bf16[2,1,512]{2,1,0:T(2,128)(2,1)}) custom-call(s32[1,24]{1,0:T(1,128)} %bitcast.37, s32[1]{0:T(128)} %bitcast.part_ref.refs_1_, s32[1]{0:T(128)} %bitcast.1.core_ref.refs_2_, ...), custom_call_target="tpu_custom_call" | custom-call | tf_op jit(solution)/shard_map/pallas_call | solution.py:456
  121.2 1.3 collective-permute-start.6
  122.5 1.3 %collective-permute-start.7 = (bf16[2,32,8,128]{3,2,1,0:T(8,128)(2,1)}, bf16[2,32,8,128]{3,2,1,0:T(8,128)(2,1)S(1)}, u32[]{:S(2)}, u32[]{:S(2)}) collective-permute-start(bf16[2,32,8,128]{3,2,1,0:T(8,128)(2,1)} %get-tuple-element.22), channel_id=1, source_target_pairs={{0,2},{1,3},{2,0},{3,1},{4,6},{5,7},{6,4},{7,5},{8,10},{9,11},{10,... | collective-permute-start | bytes 393224 | tf_op jit(solution)/shard_map/ppermute | solution.py:638
  123.8 2.0 %collective-permute-start.8 = (bf16[2,32,8,128]{3,2,1,0:T(8,128)(2,1)}, bf16[2,32,8,128]{3,2,1,0:T(8,128)(2,1)S(1)}, u32[]{:S(2)}, u32[]{:S(2)}) collective-permute-start(bf16[2,32,8,128]{3,2,1,0:T(8,128)(2,1)} %get-tuple-element.23), channel_id=1, source_target_pairs={{0,3},{1,0},{2,1},{3,2},{4,7},{5,4},{6,5},{7,6},{8,11},{9,8},{10,9... | collective-permute-start | bytes 393224 | tf_op jit(solution)/shard_map/ppermute | solution.py:638
  125.8 0.0 collective-permute-done.11
  125.8 0.6 reshape.54
  126.4 2.5 %collective-permute-done.6.rest_0_ = bf16[2,32,8,128]{3,2,1,0:T(8,128)(2,1)S(1)} collective-permute-done((bf16[2,32,8,128]{3,2,1,0:T(8,128)(2,1)}, bf16[2,32,8,128]{3,2,1,0:T(8,128)(2,1)S(1)}, u32[]{:S(2)}, u32[]{:S(2)}) %collective-permute-start.6) | collective-permute-done | bytes 131104 | tf_op jit(solution)/shard_map/ppermute | solution.py:638
  128.9 0.0 collective-permute-done.7.rest_1_
  128.9 0.5 collective-permute-done.8.rest_2_
  129.4 0.5 all-to-all-done.2
  129.9 2.1 %place.1 = bf16[768,8,128]{2,1,0:T(8,128)(2,1)} custom-call(s32[24]{0:T(128)S(1)} %copy-done.8, s32[24]{0:T(128)S(1)} %get-tuple-element.26.off_ref, s32[1]{0:T(128)} %bitcast.part_ref.refs_1_, bf16[2,32,4,2,8,128]{5,4,3,2,1,0:T(8,128)(2,1)S(1)} %bitcast.34, bf16[2,32,8,128]{3,2,1,0:T(8,128)(2,1)} %get-tuple-element.20.own_ref, ...), custom_call_target="tpu_custom_call" | custom-call | tf_op jit(solution)/shard_map/place/pallas_call | solution.py:616
  (29 shorter events, 0.1 us)
Async XLA Ops:
  3.4 19.6 %collective-permute-start = (bf16[256,512]{1,0:T(8,128)(2,1)S(1)}, bf16[256,512]{1,0:T(8,128)(2,1)S(1)}, u32[]{:S(2)}, u32[]{:S(2)}) collective-permute-start(bf16[256,512]{1,0:T(8,128)(2,1)S(1)} %get-tuple-element.18), channel_id=1, source_target_pairs={{0,1},{1,2},{2,3},{3,0},{4,5},{5,6},{6,7},{7,4},{8,9},{9,10},{10,1... | collective-permute-start | bytes 786440 | tf_op jit(solution)/shard_map/ppermute | solution.py:638
  5.5 18.0 %collective-permute-start.1 = (bf16[256,512]{1,0:T(8,128)(2,1)S(1)}, bf16[256,512]{1,0:T(8,128)(2,1)S(1)}, u32[]{:S(2)}, u32[]{:S(2)}) collective-permute-start(bf16[256,512]{1,0:T(8,128)(2,1)S(1)} %get-tuple-element.18), channel_id=1, source_target_pairs={{0,2},{1,3},{2,0},{3,1},{4,6},{5,7},{6,4},{7,5},{8,10},{9,11},{10,... | collective-permute-start | bytes 786440 | tf_op jit(solution)/shard_map/ppermute | solution.py:638
  7.9 15.6 %collective-permute-start.2 = (bf16[256,512]{1,0:T(8,128)(2,1)S(1)}, bf16[256,512]{1,0:T(8,128)(2,1)S(1)}, u32[]{:S(2)}, u32[]{:S(2)}) collective-permute-start(bf16[256,512]{1,0:T(8,128)(2,1)S(1)} %get-tuple-element.18), channel_id=1, source_target_pairs={{0,3},{1,0},{2,1},{3,2},{4,7},{5,4},{6,5},{7,6},{8,11},{9,8},{10,9... | collective-permute-start | bytes 786440 | tf_op jit(solution)/shard_map/ppermute | solution.py:638
  9.1 30.4 %all-to-all-start = ((bf16[64,40,128]{2,1,0:T(8,128)(2,1)}), bf16[64,40,128]{2,1,0:T(8,128)(2,1)S(1)}, u32[]{:S(2)}, u32[]{:S(2)}) async-start(bf16[64,40,128]{2,1,0:T(8,128)(2,1)} %bitcast.41), calls=%async_computation | async-start | bytes 1310720 | tf_op jit(solution)/shard_map/all_to_all | solution.py:659
  23.0 6.1 %copy-start.2 = (bf16[256,512]{1,0:T(8,128)(2,1)}, bf16[256,512]{1,0:T(8,128)(2,1)S(1)}, u32[]{:S(2)}) copy-start(bf16[256,512]{1,0:T(8,128)(2,1)S(1)} %collective-permute-done.rest_0_.refs_5_) | copy-start | bytes 786436
  23.0 6.0 %collective-permute-start.3 = (bf16[256,512]{1,0:T(8,128)(2,1)S(1)}, bf16[256,512]{1,0:T(8,128)(2,1)S(1)}, u32[]{:S(2)}, u32[]{:S(2)}) collective-permute-start(bf16[256,512]{1,0:T(8,128)(2,1)S(1)} %collective-permute-done.rest_0_.refs_5_), channel_id=1, source_target_pairs={{0,4},{4,0},{8,12},{12,8},{16,20},{20,16},{24,28},{28,24},{32,36},... | collective-permute-start | bytes 786440 | tf_op jit(solution)/shard_map/ppermute | solution.py:657
  23.5 5.6 %copy-start.3 = (bf16[256,512]{1,0:T(8,128)(2,1)}, bf16[256,512]{1,0:T(8,128)(2,1)S(1)}, u32[]{:S(2)}) copy-start(bf16[256,512]{1,0:T(8,128)(2,1)S(1)} %collective-permute-done.1.rest_1_.refs_6_) | copy-start | bytes 786436
  23.5 5.6 %collective-permute-start.4 = (bf16[256,512]{1,0:T(8,128)(2,1)S(1)}, bf16[256,512]{1,0:T(8,128)(2,1)S(1)}, u32[]{:S(2)}, u32[]{:S(2)}) collective-permute-start(bf16[256,512]{1,0:T(8,128)(2,1)S(1)} %collective-permute-done.1.rest_1_.refs_6_), channel_id=1, source_target_pairs={{0,4},{4,0},{8,12},{12,8},{16,20},{20,16},{24,28},{28,24},{32,36},... | collective-permute-start | bytes 786440 | tf_op jit(solution)/shard_map/ppermute | solution.py:657
  23.6 5.5 %copy-start.4 = (bf16[256,512]{1,0:T(8,128)(2,1)}, bf16[256,512]{1,0:T(8,128)(2,1)S(1)}, u32[]{:S(2)}) copy-start(bf16[256,512]{1,0:T(8,128)(2,1)S(1)} %collective-permute-done.2.rest_2_.refs_7_) | copy-start | bytes 786436
  23.6 5.5 %collective-permute-start.5 = (bf16[256,512]{1,0:T(8,128)(2,1)S(1)}, bf16[256,512]{1,0:T(8,128)(2,1)S(1)}, u32[]{:S(2)}, u32[]{:S(2)}) collective-permute-start(bf16[256,512]{1,0:T(8,128)(2,1)S(1)} %collective-permute-done.2.rest_2_.refs_7_), channel_id=1, source_target_pairs={{0,4},{4,0},{8,12},{12,8},{16,20},{20,16},{24,28},{28,24},{32,36},... | collective-permute-start | bytes 786440 | tf_op jit(solution)/shard_map/ppermute | solution.py:657
  29.0 9.3 %copy-start.5 = (bf16[256,512]{1,0:T(8,128)(2,1)}, bf16[256,512]{1,0:T(8,128)(2,1)S(1)}, u32[]{:S(2)}) copy-start(bf16[256,512]{1,0:T(8,128)(2,1)S(1)} %collective-permute-done.3.rest_3_.refs_8_) | copy-start | bytes 786436
  29.0 9.3 %copy-start.6 = (bf16[256,512]{1,0:T(8,128)(2,1)}, bf16[256,512]{1,0:T(8,128)(2,1)S(1)}, u32[]{:S(2)}) copy-start(bf16[256,512]{1,0:T(8,128)(2,1)S(1)} %collective-permute-done.4.rest_4_.refs_9_) | copy-start | bytes 786436
  29.1 9.3 %copy-start.7 = (bf16[256,512]{1,0:T(8,128)(2,1)}, bf16[256,512]{1,0:T(8,128)(2,1)S(1)}, u32[]{:S(2)}) copy-start(bf16[256,512]{1,0:T(8,128)(2,1)S(1)} %collective-permute-done.5.rest_5_.refs_10_) | copy-start | bytes 786436
  39.5 2.1 %copy-start.1 = (bf16[64,40,128]{2,1,0:T(8,128)(2,1)}, bf16[64,40,128]{2,1,0:T(8,128)(2,1)S(1)}, u32[]{:S(2)}) copy-start(bf16[64,40,128]{2,1,0:T(8,128)(2,1)S(1)} %all-to-all-done) | copy-start | bytes 1966084
  41.6 45.3 %all-to-all-start.1 = ((bf16[64,96,128]{2,1,0:T(8,128)(2,1)}), bf16[64,96,128]{2,1,0:T(8,128)(2,1)S(1)}, u32[]{:S(2)}, u32[]{:S(2)}) async-start(bf16[64,96,128]{2,1,0:T(8,128)(2,1)} %bitcast.39), calls=%async_computation.1 | async-start | bytes 3145728 | tf_op jit(solution)/shard_map/all_to_all | solution.py:669
  86.9 1.8 %copy-start = (bf16[64,96,128]{2,1,0:T(8,128)(2,1)}, bf16[64,96,128]{2,1,0:T(8,128)(2,1)S(1)}, u32[]{:S(2)}) copy-start(bf16[64,96,128]{2,1,0:T(8,128)(2,1)S(1)} %all-to-all-done.1) | copy-start | bytes 4718596
  88.7 41.2 %all-to-all-start.2 = ((bf16[256,16,128]{2,1,0:T(8,128)(2,1)}), bf16[256,16,128]{2,1,0:T(8,128)(2,1)S(1)}, u32[]{:S(2)}, u32[]{:S(2)}) async-start(bf16[256,16,128]{2,1,0:T(8,128)(2,1)} %bitcast.40), calls=%async_computation.2 | async-start | bytes 2097152 | tf_op jit(solution)/shard_map/all_to_all | solution.py:689
  99.0 7.8 %copy-start.9 = (bf16[4,1,512]{2,1,0:T(2,128)(2,1)S(1)}, bf16[4,1,512]{2,1,0:T(2,128)(2,1)}, u32[]{:S(2)}) copy-start(bf16[4,1,512]{2,1,0:T(2,128)(2,1)} %get-tuple-element.25) | copy-start | bytes 12292
  107.6 5.0 %collective-permute-start.9 = (bf16[6,128]{1,0:T(8,128)(2,1)S(1)}, bf16[6,128]{1,0:T(8,128)(2,1)S(1)}, u32[]{:S(2)}, u32[]{:S(2)}) collective-permute-start(bf16[6,128]{1,0:T(8,128)(2,1)S(1)} %bitcast.48), channel_id=1, source_target_pairs={{0,1},{1,2},{2,3},{3,0},{4,5},{5,6},{6,7},{7,4},{8,9},{9,10},{10,1... | collective-permute-start | bytes 4616 | tf_op jit(solution)/shard_map/ppermute | solution.py:638
  109.0 4.2 %collective-permute-start.10 = (bf16[6,128]{1,0:T(8,128)(2,1)S(1)}, bf16[6,128]{1,0:T(8,128)(2,1)S(1)}, u32[]{:S(2)}, u32[]{:S(2)}) collective-permute-start(bf16[6,128]{1,0:T(8,128)(2,1)S(1)} %bitcast.47), channel_id=1, source_target_pairs={{0,2},{1,3},{2,0},{3,1},{4,6},{5,7},{6,4},{7,5},{8,10},{9,11},{10,... | collective-permute-start | bytes 4616 | tf_op jit(solution)/shard_map/ppermute | solution.py:638
  111.4 14.4 %collective-permute-start.11 = (bf16[6,128]{1,0:T(8,128)(2,1)S(1)}, bf16[6,128]{1,0:T(8,128)(2,1)S(1)}, u32[]{:S(2)}, u32[]{:S(2)}) collective-permute-start(bf16[6,128]{1,0:T(8,128)(2,1)S(1)} %bitcast.46), channel_id=1, source_target_pairs={{0,3},{1,0},{2,1},{3,2},{4,7},{5,4},{6,5},{7,6},{8,11},{9,8},{10,9... | collective-permute-start | bytes 4616 | tf_op jit(solution)/shard_map/ppermute | solution.py:638
  113.3 16.6 %copy-start.8 = (s32[24]{0:T(128)S(1)}, s32[24]{0:T(128)}, u32[]{:S(2)}) copy-start(s32[24]{0:T(128)} %get-tuple-element.27.len_ref) | copy-start | bytes 292
  121.2 7.7 %collective-permute-start.6 = (bf16[2,32,8,128]{3,2,1,0:T(8,128)(2,1)}, bf16[2,32,8,128]{3,2,1,0:T(8,128)(2,1)S(1)}, u32[]{:S(2)}, u32[]{:S(2)}) collective-permute-start(bf16[2,32,8,128]{3,2,1,0:T(8,128)(2,1)} %get-tuple-element.21), channel_id=1, source_target_pairs={{0,1},{1,2},{2,3},{3,0},{4,5},{5,6},{6,7},{7,4},{8,9},{9,10},{10,1... | collective-permute-start | bytes 393224 | tf_op jit(solution)/shard_map/ppermute | solution.py:638
  122.5 6.4 %collective-permute-start.7 = (bf16[2,32,8,128]{3,2,1,0:T(8,128)(2,1)}, bf16[2,32,8,128]{3,2,1,0:T(8,128)(2,1)S(1)}, u32[]{:S(2)}, u32[]{:S(2)}) collective-permute-start(bf16[2,32,8,128]{3,2,1,0:T(8,128)(2,1)} %get-tuple-element.22), channel_id=1, source_target_pairs={{0,2},{1,3},{2,0},{3,1},{4,6},{5,7},{6,4},{7,5},{8,10},{9,11},{10,... | collective-permute-start | bytes 393224 | tf_op jit(solution)/shard_map/ppermute | solution.py:638
  123.8 5.6 %collective-permute-start.8 = (bf16[2,32,8,128]{3,2,1,0:T(8,128)(2,1)}, bf16[2,32,8,128]{3,2,1,0:T(8,128)(2,1)S(1)}, u32[]{:S(2)}, u32[]{:S(2)}) collective-permute-start(bf16[2,32,8,128]{3,2,1,0:T(8,128)(2,1)} %get-tuple-element.23), channel_id=1, source_target_pairs={{0,3},{1,0},{2,1},{3,2},{4,7},{5,4},{6,5},{7,6},{8,11},{9,8},{10,9... | collective-permute-start | bytes 393224 | tf_op jit(solution)/shard_map/ppermute | solution.py:638

commit v2 on v1

--- a/solution.py
+++ b/solution.py
@@ -249,18 +249,20 @@
     )(starts, part, core, tokens, w_own, owner, hist_len, recv_offset)
 
 
-def head_order(part):
-    return [part] + [(part + HEADS - s) % HEADS for s in range(1, HEADS)]
-
-
-def mix(low_is_near, half_rows, first, near, far, w_out_of, x_rows):
+def head_order(part, core):
+    down, up = (part + HEADS - 1) % HEADS, (part + 1) % HEADS
+    first = core == 0
+    return [part, jnp.where(first, down, up), jnp.where(first, up, down), (part + 2) % HEADS]
+
+
+def mix(low_is_near, half_rows, first, whole, halves, w_out_of, x_rows):
     low = half_rows[:, : D // 2]
     high = half_rows[:, D // 2 :]
     parts = [jnp.where(low_is_near, low, high), jnp.where(low_is_near, high, low)]
     users = half_rows.shape[0] // WIN
     heads, gates = [first[0]], [first[1]]
-    for near_ref, far_ref in zip(near, far):
-        u, v, q, k = project(parts, [near_ref[...], far_ref[...]])
+    for rows, refs in (([half_rows], whole[:1]), ([half_rows], whole[1:]), (parts, halves)):
+        u, v, q, k = project(rows, [ref[...] for ref in refs])
         gates.append(u)
         heads.append(attend_users(users, q, k, v))
     total = jnp.sum(heads[0] + heads[1] + (heads[2] + heads[3]), axis=1, keepdims=True)
@@ -292,21 +294,20 @@
     return jnp.sum(jnp.where(pick, tile.astype(F32), 0.0), axis=0, keepdims=True).astype(BF16)
 
 
-def w_out_copies(part, w_out_ref, w_out_s, sem):
+def w_out_copies(part, core, w_out_ref, w_out_s, sem):
     return [
         pltpu.make_async_copy(
             w_out_ref.at[pl.ds(h * HEAD, HEAD)], w_out_s.at[pl.ds(s * HEAD, HEAD)], sem.at[s]
         )
-        for s, h in enumerate(head_order(part))
+        for s, h in enumerate(head_order(part, core))
     ]
 
 
 def layer_kernel(
     start_ref, len_ref, part_ref, core_ref, tokens_ref, half_hbm, att_hbm, gate_hbm, *rest
 ):
-    near, far = rest[: HEADS - 1], rest[HEADS - 1 : 2 * HEADS - 2]
-    w_out_ref, out_ref, state_ref = rest[2 * HEADS - 2 : 2 * HEADS + 1]
-    x_s, half_s, att_s, gate_s, w_out_s, out_s, sem_in, sem_w, sem_out = rest[2 * HEADS + 1 :]
+    whole, halves, (w_out_ref, out_ref, state_ref) = rest[:2], rest[2:4], rest[4:7]
+    x_s, half_s, att_s, gate_s, w_out_s, out_s, sem_in, sem_w, sem_out = rest[7:]
     low_is_near = core_ref[0] == 0
     first_id = part_ref[0] * MINE + RAW
 
@@ -318,7 +319,7 @@
             for j, (a, b) in enumerate(pairs)
         ] + token_copies(tokens_ref, start_ref[0, first_id + i], x_s, i * WIN, sem_in.at[i])
 
-    weights = w_out_copies(part_ref[0], w_out_ref, w_out_s, sem_w)
+    weights = w_out_copies(part_ref[0], core_ref[0], w_out_ref, w_out_s, sem_w)
 
     def sends(i):
         at = (i % HALVES, slice(None), pl.ds((i // HALVES) * N_MP, N_MP))
@@ -350,8 +351,8 @@
             low_is_near,
             half_s[rows, :],
             (att_s[rows, :], gate_s[rows, :]),
-            near,
-            far,
+            whole,
+            halves,
             w_out_of,
             lambda: x_s[rows, :],
         )
@@ -377,14 +378,14 @@
         sends(i).wait()
 
 
-def layer(tokens, starts, lengths, part, core, kept, near, far, w_out):
+def layer(tokens, starts, lengths, part, core, kept, weights, w_out):
     message = (HALVES, GROUPS, MSG, TILE, HEAD)
     return pl.pallas_call(
         layer_kernel,
         grid_spec=pltpu.PrefetchScalarGridSpec(
             num_scalar_prefetch=4,
             grid=(1,),
-            in_specs=[in_hbm()] * 4 + [in_vmem()] * (2 * HEADS - 2) + [in_hbm()],
+            in_specs=[in_hbm()] * 4 + [in_vmem()] * 4 + [in_hbm()],
             out_specs=[in_hbm(), in_vmem()],
             scratch_shapes=[
                 pltpu.VMEM((DONE * WIN, D), BF16),
@@ -403,14 +404,13 @@
             jax.ShapeDtypeStruct((DONE, 1, D), BF16),
         ],
         name="layer",
-    )(starts, lengths, part, core, tokens, *kept, *map(keep, near), *map(keep, far), w_out)
+    )(starts, lengths, part, core, tokens, *kept, *map(keep, weights), w_out)
 
 
 def raw_kernel(first_tile, len_ref, part_ref, core_ref, src_ref, w_own_ref, *rest):
-    near, far = rest[: HEADS - 1], rest[HEADS - 1 : 2 * HEADS - 2]
-    w_out_ref = rest[2 * HEADS - 2]
-    pieces = rest[2 * HEADS - 1 : 2 * HEADS - 1 + N_MP]
-    state_ref, x_s, w_out_s, mixed_s, sem_x, sem_w = rest[2 * HEADS - 1 + N_MP :]
+    whole, halves, w_out_ref = rest[:2], rest[2:4], rest[4]
+    pieces = rest[5 : 5 + N_MP]
+    state_ref, x_s, w_out_s, mixed_s, sem_x, sem_w = rest[5 + N_MP :]
     part = part_ref[0]
     lengths = [len_ref[0, part * MINE + k] for k in range(RAW)]
     loads = [
@@ -419,7 +419,7 @@
         )
         for k in range(RAW)
     ]
-    weights = w_out_copies(part, w_out_ref, w_out_s, sem_w)
+    weights = w_out_copies(part, core_ref[0], w_out_ref, w_out_s, sem_w)
     for copy in loads + weights:
         copy.start()
     for copy in loads:
@@ -437,7 +437,7 @@
         return w_out_s[...]
 
     both = mix(
-        core_ref[0] == 0, half, (attend_users(RAW, q, k, v), u), near, far, w_out_of, x_rows
+        core_ref[0] == 0, half, (attend_users(RAW, q, k, v), u), whole, halves, w_out_of, x_rows
     )
     for k in range(RAW):
         mixed = live_rows(both[k * WIN : (k + 1) * WIN], lengths[k])
@@ -451,14 +451,14 @@
         pieces[s][...] = mixed_s[(part + s) % N_MP]
 
 
-def raw_layer(source, first_tile, lengths, part, core, w_own, near, far, w_out):
+def raw_layer(source, first_tile, lengths, part, core, w_own, weights, w_out):
     piece = jax.ShapeDtypeStruct((RAW, GROUPS, TILE, HEAD), BF16)
     outs = pl.pallas_call(
         lambda *refs: raw_kernel(first_tile, *refs),
         grid_spec=pltpu.PrefetchScalarGridSpec(
             num_scalar_prefetch=3,
             grid=(1,),
-            in_specs=[in_hbm()] + [in_vmem()] * (2 * HEADS - 1) + [in_hbm()],
+            in_specs=[in_hbm()] + [in_vmem()] * 5 + [in_hbm()],
             out_specs=[in_vmem()] * (N_MP + 1),
             scratch_shapes=[
                 pltpu.VMEM((RAW, GROUPS, N_MP, TILE, HEAD), BF16),
@@ -469,7 +469,7 @@
             ],
         ),
         out_shape=[piece] * N_MP + [jax.ShapeDtypeStruct((RAW, 1, D), BF16)],
-    )(lengths, part, core, source, w_own, *near, *far, w_out)
+    )(lengths, part, core, source, w_own, *weights, w_out)
     return outs[:N_MP], outs[N_MP]
 
 
@@ -650,18 +650,23 @@
     raw, mine_rows = pack(
         tokens, block_start, part_1, core_1, w_uvqk, owner, hist_len, recv_offset
     )
-    near, far = [], []
-    for s in range(1, N_MP):
-        near.append(along_mp(mine_rows, s))
-    for s in range(1, N_MP):
-        far.append(lax.ppermute(near[s - 1], "dp", [(i, i ^ 1) for i in range(N_DP)]))
-
+    swap = [(i, i ^ 1) for i in range(N_DP)]
+    ring = [
+        (d * N_MP + m, d * N_MP + (m + (1 if d % 2 == 0 else N_MP - 1)) % N_MP)
+        for d in range(N_DP)
+        for m in range(N_MP)
+    ]
+    side = lax.ppermute(w_uvqk, ("dp", "mp"), ring)
+    across = along_mp(mine_rows, 2)
+    other_side = lax.ppermute(side, "dp", swap)
+    other_across = lax.ppermute(across, "dp", swap)
+    weights = (side, other_side, across, other_across)
     raw_in = lax.all_to_all(
         raw.reshape(N_DP, RAW_MSG * TILE, HEAD), "dp", 0, 0, axis_index_groups=[SEATS], tiled=True
     ).reshape(N_DP, RAW_MSG, TILE, HEAD)
     kept = own_head(tokens, block_start, part_1, w_uvqk)
     message, last = layer(
-        tokens, block_start, hist_len, part_1, core_1, kept, near, far, w_out
+        tokens, block_start, hist_len, part_1, core_1, kept, weights, w_out
     )
     message = merge(
         raw_in, (first + half)[None], message.reshape(N_DP, MSG, TILE, HEAD)
@@ -671,7 +676,7 @@
     ).reshape(N_DP, MSG, TILE, HEAD)
     _, raw_last = raw_layer(
         raw.reshape(N_DP, RAW_MSG, TILE, HEAD), 0, hist_len, part_1, core_1,
-        w_uvqk, near, far, w_out,
+        w_uvqk, weights, w_out,
     )
 
     table = raw_in[:, N_MP, 0, :].astype(jnp.int32)
@@ -692,7 +697,7 @@
     )
     pieces, _ = raw_layer(
         spread, ROUND * N_MP, recv_len[None], part_1, core_1,
-        w_uvqk, near, far, w_out,
+        w_uvqk, weights, w_out,
     )
     pieces = [pieces[0]] + [along_mp(pieces[s], s) for s in range(1, N_MP)]
     packed = place(

time: 134 us -> 132 us (0.985)
  starting transfers between devices: 49.6 us -> 47.4 us
    ppermute x9 -> x7, starting transfers between devices: 15.3 us -> 10.2 us  [along_mp(): return lax.ppermute(array, 'mp', [(i, (i + s) % N_MP) for i in range(N_MP)])]
    ppermute x3, starting transfers between devices: 1 us -> 3.98 us  [the longest x1 3.37 us: per_device(): side = lax.ppermute(w_uvqk, ('dp', 'mp'), ring)]
    ppermute x9 -> x7, waiting for transfers between devices: 3.62 us -> 3.6 us  [along_mp(): return lax.ppermute(array, 'mp', [(i, (i + s) % N_MP) for i in range(N_MP)])]
  transfers between devices with their start and end apart: 15 -> 13, of which waited for: 6 -> 6; matrix products, arithmetic and copies ran while one was open for 3% -> 3% of each run, Pallas kernels for 23% -> 25%
where the time goes in v2:
time: 132 us; the launch traced here: 130 us
  starting transfers between devices  47.4 us (36%)
  waiting for transfers between devices  39 us (30%)
  Pallas kernels  38.7 us (29%)
  other arithmetic  2.45 us (2%)
  local copies, waits for them, and re-layouts  1.56 us (1%)
    all_to_all x1, waiting for transfers between devices, per_device(): lax.all_to_all(message.reshape(N_DP, MSG * TILE, HEAD), 'dp', 0, 0, axis_...  33.3 us
    pallas_call x2, Pallas kernels, raw_layer(): pl.pallas_call(lambda *refs: raw_kernel(first_tile, *refs), grid_spec=plt...  15.8 us
    all_to_all x1, starting transfers between devices, per_device(): lax.all_to_all(raw.reshape(N_DP, RAW_MSG * TILE, HEAD), 'dp', 0, 0, axis_...  14.2 us
    ppermute x7, starting transfers between devices, along_mp(): return lax.ppermute(array, 'mp', [(i, (i + s) % N_MP) for i in range(N_MP)])  10.2 us
    all_to_all x1, starting transfers between devices, per_device(): lax.all_to_all(sorted_rows.reshape(N_DP * N_MP, ROUND * TILE, HEAD), ('dp...  9.71 us
    all_to_all x1, starting transfers between devices, per_device(): lax.all_to_all(message.reshape(N_DP, MSG * TILE, HEAD), 'dp', 0, 0, axis_...  9.34 us
    pallas_call x1, Pallas kernels, layer(): pl.pallas_call(layer_kernel, grid_spec=pltpu.PrefetchScalarGridSpec(num_s...  9.26 us
    pallas_call x1, Pallas kernels, own_head(): pl.pallas_call(own_head_kernel, grid_spec=pltpu.PrefetchScalarGridSpec(nu...  4.97 us
  transfers between devices with their start and end apart: 13, of which 6 were waited for; matrix products, arithmetic and copies ran while one was open for 3% of the time, Pallas kernels for 25%

profile of v2, /device:TPU:1, one launch (start us, length us, event | category | flops | bytes accessed | tf_op | source)
XLA Modules:
  0.0 130.3 jit_solution(326821574101932129)
XLA Ops:
  0.6 3.4 %collective-permute-start = (bf16[512,512]{1,0:T(8,128)(2,1)}, bf16[512,512]{1,0:T(8,128)(2,1)S(1)}, u32[]{:S(2)}, u32[]{:S(2)}) collective-permute-start(bf16[512,512]{1,0:T(8,128)(2,1)} %refs_4_.3), channel_id=1, source_target_pairs={{0,1},{1,2},{2,3},{3,0},{4,7},{5,4},{6,5},{7,6},{8,9},{9,10},{10,1... | collective-permute-start | bytes 1572872 | tf_op jit(solution)/shard_map/ppermute | solution.py:659
  4.0 2.7 %pack.1 = (bf16[2,32,5,8,128]{4,3,2,1,0:T(8,128)(2,1)}, bf16[256,512]{1,0:T(8,128)(2,1)S(1)}) custom-call(s32[1,24]{1,0:T(1,128)} %start_ref.5, s32[1]{0:T(128)} %bitcast.part_ref.refs_1_, s32[1]{0:T(128)} %bitcast.1.core_ref.refs_2_, bf16[6144,512]{1,0:T(8,128)(2,1)} %tokens_ref.5, bf16[512,512]{1,0:T(8,128)(2,1)} %refs_4_.3, s32[1,24]{1,0:T(1,128)} %owner_ref.1, ...), custom_call_target="tpu_custom_call" | custom-call | tf_op jit(solution)/shard_map/pack/pallas_call | solution.py:229
  6.7 0.6 collective-permute-start.2
  7.3 14.2 %all-to-all-start = ((bf16[64,40,128]{2,1,0:T(8,128)(2,1)}), bf16[64,40,128]{2,1,0:T(8,128)(2,1)S(1)}, u32[]{:S(2)}, u32[]{:S(2)}) async-start(bf16[64,40,128]{2,1,0:T(8,128)(2,1)} %bitcast.41), calls=%async_computation | async-start | bytes 1310720 | tf_op jit(solution)/shard_map/all_to_all | solution.py:664
  21.6 0.0 collective-permute-done.2.rest_2_.refs_7_
  21.6 0.5 collective-permute-start.3
  22.1 0.0 collective-permute-done.rest_0_.refs_5_
  22.1 0.1 collective-permute-start.1
  22.2 5.0 %own_head.1 = (bf16[1024,512]{1,0:T(8,128)(2,1)}, f32[1024,128]{1,0:T(8,128)}, bf16[1024,128]{1,0:T(8,128)(2,1)}) custom-call(s32[1,24]{1,0:T(1,128)} %start_ref.5, s32[1]{0:T(128)} %bitcast.part_ref.refs_1_, bf16[6144,512]{1,0:T(8,128)(2,1)} %tokens_ref.5, bf16[512,512]{1,0:T(8,128)(2,1)} %refs_4_.3), custom_call_target="tpu_custom_call" | custom-call | flops 17179869184 | bytes 4194304 | tf_op jit(solution)/shard_map/own_head/pallas_call | solution.py:158
  27.2 0.0 collective-permute-done.3.rest_3_.refs_8_
  27.2 0.0 copy-start.5
  27.2 0.0 collective-permute-done.1.rest_1_.refs_6_
  27.3 9.3 %layer.1 = (bf16[2,32,12,8,128]{4,3,2,1,0:T(8,128)(2,1)}, bf16[4,1,512]{2,1,0:T(2,128)(2,1)}) custom-call(s32[1,24]{1,0:T(1,128)} %start_ref.5, s32[1,24]{1,0:T(1,128)} %refs_0_.1, s32[1]{0:T(128)} %bitcast.part_ref.refs_1_, s32[1]{0:T(128)} %bitcast.1.core_ref.refs_2_, bf16[6144,512]{1,0:T(8,128)(2,1)} %tokens_ref.5, ...), custom_call_target="tpu_custom_call" | custom-call | tf_op jit(solution)/shard_map/layer/pallas_call | solution.py:383
  36.5 0.0 copy-done.5
  36.5 0.0 copy-done.2
  36.6 1.6 %all-to-all-done = bf16[64,40,128]{2,1,0:T(8,128)(2,1)S(1)} async-done(((bf16[64,40,128]{2,1,0:T(8,128)(2,1)}), bf16[64,40,128]{2,1,0:T(8,128)(2,1)S(1)}, u32[]{:S(2)}, u32[]{:S(2)}) %all-to-all-start) | async-done | bytes 655392 | tf_op jit(solution)/shard_map/all_to_all | solution.py:664
  38.1 2.1 %merge.1 = bf16[64,12,8,128]{3,2,1,0:T(8,128)(2,1)} custom-call(s32[1]{0:T(128)} %bitcast.6.first_ref, bf16[64,5,8,128]{3,2,1,0:T(8,128)(2,1)S(1)} %bitcast.35, bf16[64,12,8,128]{3,2,1,0:T(8,128)(2,1)} %bitcast.38), custom_call_target="tpu_custom_call", output_to_operand_aliasing={{}: (2, {})} | custom-call | tf_op jit(solution)/shard_map/merge/pallas_call | solution.py:497
  40.2 0.0 copy-done.3
  40.3 9.3 %all-to-all-start.1 = ((bf16[64,96,128]{2,1,0:T(8,128)(2,1)}), bf16[64,96,128]{2,1,0:T(8,128)(2,1)S(1)}, u32[]{:S(2)}, u32[]{:S(2)}) async-start(bf16[64,96,128]{2,1,0:T(8,128)(2,1)} %bitcast.39), calls=%async_computation.1 | async-start | bytes 3145728 | tf_op jit(solution)/shard_map/all_to_all | solution.py:674
  49.6 0.9 slice_convert_fusion
  50.5 0.7 fusion
  51.2 0.1 constant_dynamic-slice_fusion.4
  51.3 0.1 slice.19
  51.4 0.1 copy.12
  51.4 0.1 select_reduce_fusion
  51.6 0.6 reshape.45.from_ref
  52.2 33.3 %all-to-all-done.1 = bf16[64,96,128]{2,1,0:T(8,128)(2,1)S(1)} async-done(((bf16[64,96,128]{2,1,0:T(8,128)(2,1)}), bf16[64,96,128]{2,1,0:T(8,128)(2,1)S(1)}, u32[]{:S(2)}, u32[]{:S(2)}) %all-to-all-start.1) | async-done | bytes 1572896 | tf_op jit(solution)/shard_map/all_to_all | solution.py:674
  85.5 1.7 %regroup.1 = bf16[64,4,2,8,128]{4,3,2,1,0:T(8,128)(2,1)} custom-call(s32[128]{0:T(128)} %reshape.45.from_ref, bf16[64,12,8,128]{3,2,1,0:T(8,128)(2,1)S(1)} %bitcast.32), custom_call_target="tpu_custom_call" | custom-call | tf_op jit(solution)/shard_map/regroup/pallas_call | solution.py:541
  87.3 0.0 copy-done
  87.3 9.7 %all-to-all-start.2 = ((bf16[256,16,128]{2,1,0:T(8,128)(2,1)}), bf16[256,16,128]{2,1,0:T(8,128)(2,1)S(1)}, u32[]{:S(2)}, u32[]{:S(2)}) async-start(bf16[256,16,128]{2,1,0:T(8,128)(2,1)} %bitcast.40), calls=%async_computation.2 | async-start | bytes 2097152 | tf_op jit(solution)/shard_map/all_to_all | solution.py:694
  97.1 7.8 %shard_map.87 = (bf16[2,32,8,128]{3,2,1,0:T(8,128)(2,1)}, bf16[2,32,8,128]{3,2,1,0:T(8,128)(2,1)}, bf16[2,32,8,128]{3,2,1,0:T(8,128)(2,1)}, bf16[2,32,8,128]{3,2,1,0:T(8,128)(2,1)}, bf16[2,1,512]{2,1,0:T(2,128)(2,1)}) custom-call(s32[1,24]{1,0:T(1,128)} %refs_0_.1, s32[1]{0:T(128)} %bitcast.part_ref.refs_1_, s32[1]{0:T(128)} %bitcast.1.core_ref.refs_2_, ...), custom_call_target="tpu_custom_call" | custom-call | tf_op jit(solution)/shard_map/pallas_call | solution.py:456
  105.0 0.7 maximum_reduce_fusion
  105.8 1.4 %collective-permute-start.7 = (bf16[6,128]{1,0:T(8,128)(2,1)S(1)}, bf16[6,128]{1,0:T(8,128)(2,1)S(1)}, u32[]{:S(2)}, u32[]{:S(2)}) collective-permute-start(bf16[6,128]{1,0:T(8,128)(2,1)S(1)} %bitcast.48), channel_id=1, source_target_pairs={{0,1},{1,2},{2,3},{3,0},{4,5},{5,6},{6,7},{7,4},{8,9},{9,10},{10,1... | collective-permute-start | bytes 4616 | tf_op jit(solution)/shard_map/ppermute | solution.py:638
  107.2 2.4 %collective-permute-start.8 = (bf16[6,128]{1,0:T(8,128)(2,1)S(1)}, bf16[6,128]{1,0:T(8,128)(2,1)S(1)}, u32[]{:S(2)}, u32[]{:S(2)}) collective-permute-start(bf16[6,128]{1,0:T(8,128)(2,1)S(1)} %bitcast.47), channel_id=1, source_target_pairs={{0,2},{1,3},{2,0},{3,1},{4,6},{5,7},{6,4},{7,5},{8,10},{9,11},{10,... | collective-permute-start | bytes 4616 | tf_op jit(solution)/shard_map/ppermute | solution.py:638
  109.6 1.2 collective-permute-start.9
  110.8 0.0 collective-permute-done.7
  110.8 0.6 collective-permute-done.8
  111.4 8.0 %shard_map.86 = (bf16[2,32,8,128]{3,2,1,0:T(8,128)(2,1)}, bf16[2,32,8,128]{3,2,1,0:T(8,128)(2,1)}, bf16[2,32,8,128]{3,2,1,0:T(8,128)(2,1)}, bf16[2,32,8,128]{3,2,1,0:T(8,128)(2,1)}, bf16[2,1,512]{2,1,0:T(2,128)(2,1)}) custom-call(s32[1,24]{1,0:T(1,128)} %bitcast.37, s32[1]{0:T(128)} %bitcast.part_ref.refs_1_, s32[1]{0:T(128)} %bitcast.1.core_ref.refs_2_, ...), custom_call_target="tpu_custom_call" | custom-call | tf_op jit(solution)/shard_map/pallas_call | solution.py:456
  119.4 1.3 collective-permute-start.4
  120.7 1.3 %collective-permute-start.5 = (bf16[2,32,8,128]{3,2,1,0:T(8,128)(2,1)}, bf16[2,32,8,128]{3,2,1,0:T(8,128)(2,1)S(1)}, u32[]{:S(2)}, u32[]{:S(2)}) collective-permute-start(bf16[2,32,8,128]{3,2,1,0:T(8,128)(2,1)} %get-tuple-element.22), channel_id=1, source_target_pairs={{0,2},{1,3},{2,0},{3,1},{4,6},{5,7},{6,4},{7,5},{8,10},{9,11},{10,... | collective-permute-start | bytes 393224 | tf_op jit(solution)/shard_map/ppermute | solution.py:638
  122.0 2.0 %collective-permute-start.6 = (bf16[2,32,8,128]{3,2,1,0:T(8,128)(2,1)}, bf16[2,32,8,128]{3,2,1,0:T(8,128)(2,1)S(1)}, u32[]{:S(2)}, u32[]{:S(2)}) collective-permute-start(bf16[2,32,8,128]{3,2,1,0:T(8,128)(2,1)} %get-tuple-element.23), channel_id=1, source_target_pairs={{0,3},{1,0},{2,1},{3,2},{4,7},{5,4},{6,5},{7,6},{8,11},{9,8},{10,9... | collective-permute-start | bytes 393224 | tf_op jit(solution)/shard_map/ppermute | solution.py:638
  124.0 0.0 collective-permute-done.9
  124.0 0.6 reshape.54
  124.6 2.5 %collective-permute-done.4.rest_0_ = bf16[2,32,8,128]{3,2,1,0:T(8,128)(2,1)S(1)} collective-permute-done((bf16[2,32,8,128]{3,2,1,0:T(8,128)(2,1)}, bf16[2,32,8,128]{3,2,1,0:T(8,128)(2,1)S(1)}, u32[]{:S(2)}, u32[]{:S(2)}) %collective-permute-start.4) | collective-permute-done | bytes 131104 | tf_op jit(solution)/shard_map/ppermute | solution.py:638
  127.1 0.0 collective-permute-done.5.rest_1_
  127.1 0.5 collective-permute-done.6.rest_2_
  127.5 0.5 all-to-all-done.2
  128.0 2.1 %place.1 = bf16[768,8,128]{2,1,0:T(8,128)(2,1)} custom-call(s32[24]{0:T(128)S(1)} %copy-done.6, s32[24]{0:T(128)S(1)} %get-tuple-element.26.off_ref, s32[1]{0:T(128)} %bitcast.part_ref.refs_1_, bf16[2,32,4,2,8,128]{5,4,3,2,1,0:T(8,128)(2,1)S(1)} %bitcast.34, bf16[2,32,8,128]{3,2,1,0:T(8,128)(2,1)} %get-tuple-element.20.own_ref, ...), custom_call_target="tpu_custom_call" | custom-call | tf_op jit(solution)/shard_map/place/pallas_call | solution.py:616
  (21 shorter events, 0.1 us)
Async XLA Ops:
  0.6 21.5 %collective-permute-start = (bf16[512,512]{1,0:T(8,128)(2,1)}, bf16[512,512]{1,0:T(8,128)(2,1)S(1)}, u32[]{:S(2)}, u32[]{:S(2)}) collective-permute-start(bf16[512,512]{1,0:T(8,128)(2,1)} %refs_4_.3), channel_id=1, source_target_pairs={{0,1},{1,2},{2,3},{3,0},{4,7},{5,4},{6,5},{7,6},{8,9},{9,10},{10,1... | collective-permute-start | bytes 1572872 | tf_op jit(solution)/shard_map/ppermute | solution.py:659
  6.7 14.9 %collective-permute-start.2 = (bf16[256,512]{1,0:T(8,128)(2,1)S(1)}, bf16[256,512]{1,0:T(8,128)(2,1)S(1)}, u32[]{:S(2)}, u32[]{:S(2)}) collective-permute-start(bf16[256,512]{1,0:T(8,128)(2,1)S(1)} %get-tuple-element.18), channel_id=1, source_target_pairs={{0,2},{1,3},{2,0},{3,1},{4,6},{5,7},{6,4},{7,5},{8,10},{9,11},{10,... | collective-permute-start | bytes 786440 | tf_op jit(solution)/shard_map/ppermute | solution.py:638
  7.3 30.8 %all-to-all-start = ((bf16[64,40,128]{2,1,0:T(8,128)(2,1)}), bf16[64,40,128]{2,1,0:T(8,128)(2,1)S(1)}, u32[]{:S(2)}, u32[]{:S(2)}) async-start(bf16[64,40,128]{2,1,0:T(8,128)(2,1)} %bitcast.41), calls=%async_computation | async-start | bytes 1310720 | tf_op jit(solution)/shard_map/all_to_all | solution.py:664
  21.6 5.7 %copy-start.4 = (bf16[256,512]{1,0:T(8,128)(2,1)}, bf16[256,512]{1,0:T(8,128)(2,1)S(1)}, u32[]{:S(2)}) copy-start(bf16[256,512]{1,0:T(8,128)(2,1)S(1)} %collective-permute-done.2.rest_2_.refs_7_) | copy-start | bytes 786436
  21.6 5.6 %collective-permute-start.3 = (bf16[256,512]{1,0:T(8,128)(2,1)S(1)}, bf16[256,512]{1,0:T(8,128)(2,1)S(1)}, u32[]{:S(2)}, u32[]{:S(2)}) collective-permute-start(bf16[256,512]{1,0:T(8,128)(2,1)S(1)} %collective-permute-done.2.rest_2_.refs_7_), channel_id=1, source_target_pairs={{0,4},{4,0},{8,12},{12,8},{16,20},{20,16},{24,28},{28,24},{32,36},... | collective-permute-start | bytes 786440 | tf_op jit(solution)/shard_map/ppermute | solution.py:662
  22.1 5.2 %copy-start.1 = (bf16[512,512]{1,0:T(8,128)(2,1)}, bf16[512,512]{1,0:T(8,128)(2,1)S(1)}, u32[]{:S(2)}) copy-start(bf16[512,512]{1,0:T(8,128)(2,1)S(1)} %collective-permute-done.rest_0_.refs_5_) | copy-start | bytes 1572868
  22.1 5.1 %collective-permute-start.1 = (bf16[512,512]{1,0:T(8,128)(2,1)S(1)}, bf16[512,512]{1,0:T(8,128)(2,1)S(1)}, u32[]{:S(2)}, u32[]{:S(2)}) collective-permute-start(bf16[512,512]{1,0:T(8,128)(2,1)S(1)} %collective-permute-done.rest_0_.refs_5_), channel_id=1, source_target_pairs={{0,4},{4,0},{8,12},{12,8},{16,20},{20,16},{24,28},{28,24},{32,36},... | collective-permute-start | bytes 1572872 | tf_op jit(solution)/shard_map/ppermute | solution.py:661
  27.2 9.3 %copy-start.5 = (bf16[256,512]{1,0:T(8,128)(2,1)}, bf16[256,512]{1,0:T(8,128)(2,1)S(1)}, u32[]{:S(2)}) copy-start(bf16[256,512]{1,0:T(8,128)(2,1)S(1)} %collective-permute-done.3.rest_3_.refs_8_) | copy-start | bytes 786436
  27.2 9.3 %copy-start.2 = (bf16[512,512]{1,0:T(8,128)(2,1)}, bf16[512,512]{1,0:T(8,128)(2,1)S(1)}, u32[]{:S(2)}) copy-start(bf16[512,512]{1,0:T(8,128)(2,1)S(1)} %collective-permute-done.1.rest_1_.refs_6_) | copy-start | bytes 1572868
  38.1 2.1 %copy-start.3 = (bf16[64,40,128]{2,1,0:T(8,128)(2,1)}, bf16[64,40,128]{2,1,0:T(8,128)(2,1)S(1)}, u32[]{:S(2)}) copy-start(bf16[64,40,128]{2,1,0:T(8,128)(2,1)S(1)} %all-to-all-done) | copy-start | bytes 1966084
  40.3 45.3 %all-to-all-start.1 = ((bf16[64,96,128]{2,1,0:T(8,128)(2,1)}), bf16[64,96,128]{2,1,0:T(8,128)(2,1)S(1)}, u32[]{:S(2)}, u32[]{:S(2)}) async-start(bf16[64,96,128]{2,1,0:T(8,128)(2,1)} %bitcast.39), calls=%async_computation.1 | async-start | bytes 3145728 | tf_op jit(solution)/shard_map/all_to_all | solution.py:674
  85.5 1.8 %copy-start = (bf16[64,96,128]{2,1,0:T(8,128)(2,1)}, bf16[64,96,128]{2,1,0:T(8,128)(2,1)S(1)}, u32[]{:S(2)}) copy-start(bf16[64,96,128]{2,1,0:T(8,128)(2,1)S(1)} %all-to-all-done.1) | copy-start | bytes 4718596
  87.3 40.7 %all-to-all-start.2 = ((bf16[256,16,128]{2,1,0:T(8,128)(2,1)}), bf16[256,16,128]{2,1,0:T(8,128)(2,1)S(1)}, u32[]{:S(2)}, u32[]{:S(2)}) async-start(bf16[256,16,128]{2,1,0:T(8,128)(2,1)} %bitcast.40), calls=%async_computation.2 | async-start | bytes 2097152 | tf_op jit(solution)/shard_map/all_to_all | solution.py:694
  97.1 7.8 %copy-start.7 = (bf16[4,1,512]{2,1,0:T(2,128)(2,1)S(1)}, bf16[4,1,512]{2,1,0:T(2,128)(2,1)}, u32[]{:S(2)}) copy-start(bf16[4,1,512]{2,1,0:T(2,128)(2,1)} %get-tuple-element.25) | copy-start | bytes 12292
  105.8 5.0 %collective-permute-start.7 = (bf16[6,128]{1,0:T(8,128)(2,1)S(1)}, bf16[6,128]{1,0:T(8,128)(2,1)S(1)}, u32[]{:S(2)}, u32[]{:S(2)}) collective-permute-start(bf16[6,128]{1,0:T(8,128)(2,1)S(1)} %bitcast.48), channel_id=1, source_target_pairs={{0,1},{1,2},{2,3},{3,0},{4,5},{5,6},{6,7},{7,4},{8,9},{9,10},{10,1... | collective-permute-start | bytes 4616 | tf_op jit(solution)/shard_map/ppermute | solution.py:638
  107.2 4.2 %collective-permute-start.8 = (bf16[6,128]{1,0:T(8,128)(2,1)S(1)}, bf16[6,128]{1,0:T(8,128)(2,1)S(1)}, u32[]{:S(2)}, u32[]{:S(2)}) collective-permute-start(bf16[6,128]{1,0:T(8,128)(2,1)S(1)} %bitcast.47), channel_id=1, source_target_pairs={{0,2},{1,3},{2,0},{3,1},{4,6},{5,7},{6,4},{7,5},{8,10},{9,11},{10,... | collective-permute-start | bytes 4616 | tf_op jit(solution)/shard_map/ppermute | solution.py:638
  109.6 14.4 %collective-permute-start.9 = (bf16[6,128]{1,0:T(8,128)(2,1)S(1)}, bf16[6,128]{1,0:T(8,128)(2,1)S(1)}, u32[]{:S(2)}, u32[]{:S(2)}) collective-permute-start(bf16[6,128]{1,0:T(8,128)(2,1)S(1)} %bitcast.46), channel_id=1, source_target_pairs={{0,3},{1,0},{2,1},{3,2},{4,7},{5,4},{6,5},{7,6},{8,11},{9,8},{10,9... | collective-permute-start | bytes 4616 | tf_op jit(solution)/shard_map/ppermute | solution.py:638
  111.4 16.6 %copy-start.6 = (s32[24]{0:T(128)S(1)}, s32[24]{0:T(128)}, u32[]{:S(2)}) copy-start(s32[24]{0:T(128)} %get-tuple-element.27.len_ref) | copy-start | bytes 292
  119.4 7.7 %collective-permute-start.4 = (bf16[2,32,8,128]{3,2,1,0:T(8,128)(2,1)}, bf16[2,32,8,128]{3,2,1,0:T(8,128)(2,1)S(1)}, u32[]{:S(2)}, u32[]{:S(2)}) collective-permute-start(bf16[2,32,8,128]{3,2,1,0:T(8,128)(2,1)} %get-tuple-element.21), channel_id=1, source_target_pairs={{0,1},{1,2},{2,3},{3,0},{4,5},{5,6},{6,7},{7,4},{8,9},{9,10},{10,1... | collective-permute-start | bytes 393224 | tf_op jit(solution)/shard_map/ppermute | solution.py:638
  120.7 6.4 %collective-permute-start.5 = (bf16[2,32,8,128]{3,2,1,0:T(8,128)(2,1)}, bf16[2,32,8,128]{3,2,1,0:T(8,128)(2,1)S(1)}, u32[]{:S(2)}, u32[]{:S(2)}) collective-permute-start(bf16[2,32,8,128]{3,2,1,0:T(8,128)(2,1)} %get-tuple-element.22), channel_id=1, source_target_pairs={{0,2},{1,3},{2,0},{3,1},{4,6},{5,7},{6,4},{7,5},{8,10},{9,11},{10,... | collective-permute-start | bytes 393224 | tf_op jit(solution)/shard_map/ppermute | solution.py:638
  122.0 5.6 %collective-permute-start.6 = (bf16[2,32,8,128]{3,2,1,0:T(8,128)(2,1)}, bf16[2,32,8,128]{3,2,1,0:T(8,128)(2,1)S(1)}, u32[]{:S(2)}, u32[]{:S(2)}) collective-permute-start(bf16[2,32,8,128]{3,2,1,0:T(8,128)(2,1)} %get-tuple-element.23), channel_id=1, source_target_pairs={{0,3},{1,0},{2,1},{3,2},{4,7},{5,4},{6,5},{7,6},{8,11},{9,8},{10,9... | collective-permute-start | bytes 393224 | tf_op jit(solution)/shard_map/ppermute | solution.py:638
